TPU v7x, 1024 devices: a whole 4x4x32 slice. The times are simulated.
1024 devices in a mesh: gx: 16 (over y, x), gy: 64 (over z, core).
Axes of the slice: x: 4, y: 4, z: 32, core: 2. Of those that a mesh axis runs over, the one named last changes fastest.
Arguments:
- chemical_concentration: float32 [53, 512, 8192], P(None, 'gx', 'gy'), may hold values from 0.01 to 1
- thermal_scaled: float32 [512, 8192], P('gx', 'gy'), may hold values from 1 to 2.5
- tentative_flow_spread: float32 [512, 8192], P('gx', 'gy'), may hold values from -6 to 6
- substep_numbers: int32 [16, 1024], P('gx', 'gy'), may hold values from 1 to 4, as said below
- patch_holder_lookup: int32 [16, 1024], P('gx', 'gy'), may hold values from 0 to 15, as said below
- consumed_weighting: float32 [325, 53], replicated, may hold values from -0.875 to 0.875
- molar_coefficient: float32 [325, 53], replicated, may hold values from -0.15625 to 0.15625
- frequency_factor_log: float32 [325], replicated, may hold values from -1 to 1
- arrhenius_energy: float32 [325], replicated, may hold values from 0.5 to 3
- enthalpy_released: float32 [325], replicated, may hold values from -0.3125 to 0.3125
Outputs:
- chemicals_after_window: float32 [53, 512, 8192], P(None, 'gx', 'gy')
- thermal_after_window: float32 [512, 8192], P('gx', 'gy')
- scalar_potential_field: float32 [512, 8192], P('gx', 'gy')
- holder_energy_burden: float32 [16, 64], P('gx', 'gy')
Inputs may be any that keep to these rules, and one draw needn't show every extreme that they name: `substep_numbers`: every block has 4 on some tile. `patch_holder_lookup`: in each block's 16 entries every owner 0 to 15 appears exactly 1 times.
All inputs are finite; a program needn't handle non-finite values.
Results may differ from a plain program's by a relative error of at most 0.0003.
Values sent between devices are 32-bit elements; how exact they have to be, the bound alone decides.
A program may use at most 32 MiB of HBM per device.

v0:
```python
import jax
import jax.numpy as jnp
from jax import lax
from jax.sharding import PartitionSpec as P

MAXSUB = 4
LEVELS = 3
SWEEPS = 2
COARSE = 4


step_time = 0.4
relax = 0.8
high = lax.Precision.HIGHEST
group_tiles = 4


def with_halo(shard, sides, width):
    edges = {}
    for axis, dim in sides:
        size, length = (lax.axis_size(axis), shard.shape[dim])
        up = [(i, (i + 1) % size) for i in range(size - 1)]
        last = lax.slice_in_dim(shard, length - width, length, axis=dim)
        leading = lax.slice_in_dim(shard, 0, width, axis=dim)
        edges[dim] = (
            lax.ppermute(last, axis, up),
            lax.ppermute(leading, axis, [(b, a) for a, b in up]),
        )
    done = []
    for _, dim in sides:
        low, high = edges[dim]
        around = [(width, width) if d in done else (0, 0) for d in range(shard.ndim)]
        shard = jnp.concatenate([jnp.pad(low, around), shard, jnp.pad(high, around)], axis=dim)
        done.append(dim)
    return shard


def split_up(shard, dim, size):
    before, after = (shard.shape[:dim], shard.shape[dim + 1 :])
    return jnp.moveaxis(shard.reshape(*before, size, -1, *after), dim, 0)


def sent_and_summed(shard, axis, dim):
    size = lax.axis_size(axis)
    pieces = lax.all_to_all(split_up(shard, dim, size), axis, 0, 0, tiled=True)
    return jnp.sum(pieces, axis=0)


def advance_chemistry(
    spec_in,
    temp_in,
    tallies,
    consumed_weighting,
    molar_coefficient,
    frequency_factor_log,
    arrhenius_energy,
    enthalpy_released,
):
    order = jnp.argsort(-tallies, stable=True)
    inverse = jnp.argsort(order, stable=True)
    spec_now = jnp.take(spec_in, order, axis=1)
    temp_now = jnp.take(temp_in, order, axis=0)
    sorted_counts = jnp.take(tallies, order, axis=0)
    width = step_time / sorted_counts.astype(jnp.float32)
    heat_now = jnp.zeros_like(temp_now)
    for turn in range(MAXSUB):
        active = jnp.sum((sorted_counts > turn).astype(jnp.int32))
        groups = (active + group_tiles - 1) // group_tiles

        def advance(index, carry):
            spec_all, temp_all, heat_all = carry
            start = (index * group_tiles).astype(jnp.int32)
            spec_part = lax.dynamic_slice_in_dim(spec_all, start, group_tiles, 1)
            temp_part = lax.dynamic_slice_in_dim(temp_all, start, group_tiles, 0)
            heat_part = lax.dynamic_slice_in_dim(heat_all, start, group_tiles, 0)
            count_part = lax.dynamic_slice_in_dim(sorted_counts, start, group_tiles, 0)
            width_part = lax.dynamic_slice_in_dim(width, start, group_tiles, 0)
            delta = jnp.where(turn < count_part, width_part, 0.0)
            progress = jnp.einsum("rs,sbc->rbc", consumed_weighting, spec_part, precision=high)
            rates = jnp.exp(
                frequency_factor_log[:, None, None]
                - arrhenius_energy[:, None, None] / (1.0 + jnp.abs(temp_part))[None]
            )
            flux = rates * progress
            change = jnp.einsum("rs,rbc->sbc", molar_coefficient, flux, precision=high)
            release = jnp.einsum("r,rbc->bc", enthalpy_released, flux, precision=high)
            spec_part = spec_part + delta[None, :, None] * change
            temp_part = temp_part + delta[:, None] * release
            heat_part = heat_part + delta[:, None] * release
            return (
                lax.dynamic_update_slice_in_dim(spec_all, spec_part, start, 1),
                lax.dynamic_update_slice_in_dim(temp_all, temp_part, start, 0),
                lax.dynamic_update_slice_in_dim(heat_all, heat_part, start, 0),
            )

        spec_now, temp_now, heat_now = lax.fori_loop(
            0, groups, advance, (spec_now, temp_now, heat_now)
        )
    return (
        jnp.take(spec_now, inverse, axis=1),
        jnp.take(temp_now, inverse, axis=0),
        jnp.take(heat_now, inverse, axis=0),
    )


def beside_all(field):
    padded = with_halo(field, (("gx", 0), ("gy", 1)), 1)
    return padded[2:, 1:-1] + padded[:-2, 1:-1] + padded[1:-1, 2:] + padded[1:-1, :-2]


def smooth(field, rhs, scale):
    return field + relax * (scale * rhs - 4.0 * field + beside_all(field)) / 4.0


def vcycle(rhs, level):
    scale = 4.0**level
    field = jnp.zeros_like(rhs)
    if level == LEVELS - 1:
        for turn in range(COARSE):
            field = smooth(field, rhs, scale)
        return field
    for turn in range(SWEEPS):
        field = smooth(field, rhs, scale)
    resid = rhs - (4.0 * field - beside_all(field)) / scale
    leading_span, trailing_span = resid.shape
    coarse = resid.reshape(leading_span // 2, 2, trailing_span // 2, 2).mean(axis=(1, 3))
    correction = vcycle(coarse, level + 1)
    field = field + jnp.repeat(jnp.repeat(correction, 2, axis=0), 2, axis=1)
    for turn in range(SWEEPS):
        field = smooth(field, rhs, scale)
    return field


def shards(
    chemical_concentration,
    thermal_scaled,
    tentative_flow_spread,
    substep_numbers,
    patch_holder_lookup,
    consumed_weighting,
    molar_coefficient,
    frequency_factor_log,
    arrhenius_energy,
    enthalpy_released,
):
    chemical_total, leading_span, trailing_span = chemical_concentration.shape
    groups = lax.axis_size("gx")
    tiles = substep_numbers.shape[1]
    volume_total = leading_span * trailing_span
    tile_len = volume_total // tiles
    tallies = substep_numbers[0]
    owners = patch_holder_lookup[0]
    updated_chemicals, thermal_following, updated_thermal = advance_chemistry(
        chemical_concentration.reshape(chemical_total, tiles, tile_len),
        thermal_scaled.reshape(tiles, tile_len),
        tallies,
        consumed_weighting,
        molar_coefficient,
        frequency_factor_log,
        arrhenius_energy,
        enthalpy_released,
    )
    tile_sums = jnp.sum(updated_thermal * updated_thermal, axis=-1)
    onehot = (owners[:, None] == jnp.arange(groups, dtype=jnp.int32)[None, :]).astype(jnp.float32)
    shares = jnp.dot(tile_sums, onehot, precision=high)
    holder_energy_burden = (sent_and_summed(shares, "gx", 0) / volume_total).reshape(1, 1)
    chemicals_after_window = updated_chemicals.reshape(chemical_total, leading_span, trailing_span)
    thermal_after_window = thermal_following.reshape(leading_span, trailing_span)
    heat_grid = updated_thermal.reshape(leading_span, trailing_span)
    scalar_potential_field = vcycle(tentative_flow_spread + heat_grid, 0)
    return (
        chemicals_after_window,
        thermal_after_window,
        scalar_potential_field,
        holder_energy_burden,
    )


def solution(mesh):
    return jax.shard_map(
        shards,
        mesh=mesh,
        in_specs=(
            P(None, "gx", "gy"),
            P("gx", "gy"),
            P("gx", "gy"),
            P("gx", "gy"),
            P("gx", "gy"),
            P(),
            P(),
            P(),
            P(),
            P(),
        ),
        out_specs=(P(None, "gx", "gy"), P("gx", "gy"), P("gx", "gy"), P("gx", "gy")),
        check_vma=False,
    )
```

profile of v0, /device:TPU:646, one launch (start us, length us, event | category | flops | bytes accessed | tf_op | source)
XLA Modules:
  0.0 299.2 jit_solution(16181039454688431183)
XLA Ops:
  0.6 2.7 collective-permute-start
  3.4 5.2 %collective-permute-start.1 = (f32[1,128]{0,1:T(8,128)S(1)}, f32[1,128]{0,1:T(8,128)S(1)}, u32[]{:S(2)}, u32[]{:S(2)}) collective-permute-start(f32[1,128]{0,1:T(8,128)S(1)} %broadcast.238), channel_id=1, source_target_pairs={{0,64},{64,128},{128,192},{192,256},{256,320},{320,384},{384,448},... | collective-permute-start | bytes 1544 | tf_op jit(solution)/shard_map/ppermute | solution.py:26
  8.6 3.0 %collective-permute-start.2 = (f32[32,1]{0,1:T(1,128)S(1)}, f32[32,1]{0,1:T(1,128)S(1)}, u32[]{:S(2)}, u32[]{:S(2)}) collective-permute-start(f32[32,1]{0,1:T(1,128)S(1)} %broadcast.239), channel_id=1, source_target_pairs={{1,0},{2,1},{3,2},{4,3},{5,4},{6,5},{7,6},{8,7},{9,8},{10,9},{11,1... | collective-permute-start | bytes 392 | tf_op jit(solution)/shard_map/ppermute | solution.py:27
  11.6 1.9 collective-permute-start.3
  13.6 4.9 %collective-permute-start.14 = (f32[16,1]{1,0:T(8,128)S(1)}, f32[16,1]{1,0:T(8,128)S(1)}, u32[]{:S(2)}, u32[]{:S(2)}) collective-permute-start(f32[16,1]{1,0:T(8,128)S(1)} %broadcast.242), channel_id=1, source_target_pairs={{1,0},{2,1},{3,2},{4,3},{5,4},{6,5},{7,6},{8,7},{9,8},{10,9},{11,1... | collective-permute-start | bytes 200 | tf_op jit(solution)/shard_map/ppermute | solution.py:27
  32.5 14.2 %while.60 = (s32[]{:T(128)}, f32[53,16,256]{2,0,1:T(8,128)S(1)}, f32[16,256]{1,0:T(8,128)S(1)}, f32[16,256]{1,0:T(8,128)S(1)}, s32[]{:T(128)}, /*index=5*/s32[16...) while((s32[]{:T(128)}, f32[53,16,256]{2,0,1:T(8,128)S(1)}, ...), condition=%wide.wide.region_3.6_spmd, body=%wide.wide.region_2.5_spmd.sunk | while | flops 428427264 | bytes 4909603 | solution.py:96
  46.7 14.2 %while.61 = (s32[]{:T(128)}, f32[53,16,256]{2,0,1:T(8,128)S(1)}, f32[16,256]{1,0:T(8,128)S(1)}, f32[16,256]{1,0:T(8,128)S(1)}, s32[]{:T(128)}, /*index=5*/s32[16...) while((s32[]{:T(128)}, f32[53,16,256]{2,0,1:T(8,128)S(1)}, ...), condition=%wide.wide.region_6.9_spmd, body=%wide.wide.region_5.8_spmd.sunk | while | flops 428427264 | bytes 4909603 | solution.py:96
  61.0 14.2 %while.62 = (s32[]{:T(128)}, f32[53,16,256]{2,0,1:T(8,128)S(1)}, f32[16,256]{1,0:T(8,128)S(1)}, f32[16,256]{1,0:T(8,128)S(1)}, s32[]{:T(128)}, /*index=5*/s32[16...) while((s32[]{:T(128)}, f32[53,16,256]{2,0,1:T(8,128)S(1)}, ...), condition=%wide.wide.region_9.12_spmd, body=%wide.wide.region_8.11_spmd.sunk | while | flops 428427264 | bytes 4909603 | solution.py:96
  75.2 14.4 %while.63 = (s32[]{:T(128)}, f32[53,16,256]{2,0,1:T(8,128)S(1)}, f32[16,256]{1,0:T(8,128)S(1)}, f32[16,256]{1,0:T(8,128)S(1)}, s32[]{:T(128)}, /*index=5*/s32[16...) while((s32[]{:T(128)}, f32[53,16,256]{2,0,1:T(8,128)S(1)}, ...), condition=%wide.wide.region_12.15_spmd, body=%wide.wide.region_11.14_spmd.sunk | while | flops 428427264 | bytes 4909603 | solution.py:96
  91.8 7.2 %all-to-all-start = ((f32[16,1,1]{2,1,0:T(1,128)}), f32[16,1,1]{2,1,0:T(1,128)S(1)}, u32[]{:S(2)}, u32[]{:S(2)}) async-start(f32[16,1,1]{2,1,0:T(1,128)} %bitcast.33), calls=%async_computation | async-start | bytes 16384 | tf_op jit(solution)/shard_map/all_to_all | solution.py:45
  101.6 2.8 collective-permute-start.4
  104.4 5.2 %collective-permute-start.5 = (f32[1,128]{0,1:T(8,128)S(1)}, f32[1,128]{0,1:T(8,128)S(1)}, u32[]{:S(2)}, u32[]{:S(2)}) collective-permute-start(f32[1,128]{0,1:T(8,128)S(1)} %get-tuple-element.432), channel_id=1, source_target_pairs={{0,64},{64,128},{128,192},{192,256},{256,320},{320,384},{384,448},... | collective-permute-start | bytes 1544 | tf_op jit(solution)/shard_map/ppermute | solution.py:26
  111.5 2.4 collective-permute-start.7
  114.9 2.7 collective-permute-done.7
  119.9 6.0 %collective-permute-start.9 = (f32[1,128]{0,1:T(8,128)S(1)}, f32[1,128]{0,1:T(8,128)S(1)}, u32[]{:S(2)}, u32[]{:S(2)}) collective-permute-start(f32[1,128]{0,1:T(8,128)S(1)} %get-tuple-element.428), channel_id=1, source_target_pairs={{0,64},{64,128},{128,192},{192,256},{256,320},{320,384},{384,448},... | collective-permute-start | bytes 1544 | tf_op jit(solution)/shard_map/ppermute | solution.py:26
  125.9 1.9 collective-permute-start.10
  127.8 2.4 collective-permute-start.11
  135.9 6.0 %collective-permute-start.13 = (f32[1,64]{1,0:T(1,128)S(1)}, f32[1,64]{1,0:T(1,128)S(1)}, u32[]{:S(2)}, u32[]{:S(2)}) collective-permute-start(f32[1,64]{1,0:T(1,128)S(1)} %broadcast.241), channel_id=1, source_target_pairs={{0,64},{64,128},{128,192},{192,256},{256,320},{320,384},{384,448},... | collective-permute-start | bytes 776 | tf_op jit(solution)/shard_map/ppermute | solution.py:26
  141.9 2.6 collective-permute-start.26
  146.2 2.5 collective-permute-start.18
  148.7 1.9 collective-permute-start.16
  150.6 6.0 %collective-permute-start.17 = (f32[1,64]{1,0:T(1,128)S(1)}, f32[1,64]{1,0:T(1,128)S(1)}, u32[]{:S(2)}, u32[]{:S(2)}) collective-permute-start(f32[1,64]{1,0:T(1,128)S(1)} %get-tuple-element.448), channel_id=1, source_target_pairs={{0,64},{64,128},{128,192},{192,256},{256,320},{320,384},{384,448},... | collective-permute-start | bytes 776 | tf_op jit(solution)/shard_map/ppermute | solution.py:26
  156.7 1.9 collective-permute-start.19
  158.6 2.9 collective-permute-start.27
  163.0 2.6 collective-permute-start.22
  169.5 6.0 %collective-permute-start.21 = (f32[1,64]{1,0:T(1,128)S(1)}, f32[1,64]{1,0:T(1,128)S(1)}, u32[]{:S(2)}, u32[]{:S(2)}) collective-permute-start(f32[1,64]{1,0:T(1,128)S(1)} %get-tuple-element.444), channel_id=1, source_target_pairs={{0,64},{64,128},{128,192},{192,256},{256,320},{320,384},{384,448},... | collective-permute-start | bytes 776 | tf_op jit(solution)/shard_map/ppermute | solution.py:26
  175.5 1.9 collective-permute-start.24
  177.5 6.0 %collective-permute-start.25 = (f32[1,32]{1,0:T(1,128)S(1)}, f32[1,32]{1,0:T(1,128)S(1)}, u32[]{:S(2)}, u32[]{:S(2)}) collective-permute-start(f32[1,32]{1,0:T(1,128)S(1)} %broadcast.245), channel_id=1, source_target_pairs={{0,64},{64,128},{128,192},{192,256},{256,320},{320,384},{384,448},... | collective-permute-start | bytes 392 | tf_op jit(solution)/shard_map/ppermute | solution.py:26
  184.9 3.1 %collective-permute-start.30 = (f32[8,1]{1,0:T(8,128)S(1)}, f32[8,1]{1,0:T(8,128)S(1)}, u32[]{:S(2)}, u32[]{:S(2)}) collective-permute-start(f32[8,1]{1,0:T(8,128)S(1)} %get-tuple-element.458), channel_id=1, source_target_pairs={{1,0},{2,1},{3,2},{4,3},{5,4},{6,5},{7,6},{8,7},{9,8},{10,9},{11,1... | collective-permute-start | bytes 104 | tf_op jit(solution)/shard_map/ppermute | solution.py:27
  191.9 6.0 %collective-permute-start.29 = (f32[1,32]{1,0:T(1,128)S(1)}, f32[1,32]{1,0:T(1,128)S(1)}, u32[]{:S(2)}, u32[]{:S(2)}) collective-permute-start(f32[1,32]{1,0:T(1,128)S(1)} %get-tuple-element.460), channel_id=1, source_target_pairs={{0,64},{64,128},{128,192},{192,256},{256,320},{320,384},{384,448},... | collective-permute-start | bytes 392 | tf_op jit(solution)/shard_map/ppermute | solution.py:26
  199.4 4.0 %collective-permute-start.34 = (f32[8,1]{1,0:T(8,128)S(1)}, f32[8,1]{1,0:T(8,128)S(1)}, u32[]{:S(2)}, u32[]{:S(2)}) collective-permute-start(f32[8,1]{1,0:T(8,128)S(1)} %get-tuple-element.454), channel_id=1, source_target_pairs={{1,0},{2,1},{3,2},{4,3},{5,4},{6,5},{7,6},{8,7},{9,8},{10,9},{11,1... | collective-permute-start | bytes 104 | tf_op jit(solution)/shard_map/ppermute | solution.py:27
  205.3 1.9 collective-permute-start.32
  207.2 6.0 %collective-permute-start.33 = (f32[1,32]{1,0:T(1,128)S(1)}, f32[1,32]{1,0:T(1,128)S(1)}, u32[]{:S(2)}, u32[]{:S(2)}) collective-permute-start(f32[1,32]{1,0:T(1,128)S(1)} %get-tuple-element.456), channel_id=1, source_target_pairs={{0,64},{64,128},{128,192},{192,256},{256,320},{320,384},{384,448},... | collective-permute-start | bytes 392 | tf_op jit(solution)/shard_map/ppermute | solution.py:26
  214.7 4.0 %collective-permute-start.38 = (f32[8,1]{1,0:T(8,128)S(1)}, f32[8,1]{1,0:T(8,128)S(1)}, u32[]{:S(2)}, u32[]{:S(2)}) collective-permute-start(f32[8,1]{1,0:T(8,128)S(1)} %get-tuple-element.450), channel_id=1, source_target_pairs={{1,0},{2,1},{3,2},{4,3},{5,4},{6,5},{7,6},{8,7},{9,8},{10,9},{11,1... | collective-permute-start | bytes 104 | tf_op jit(solution)/shard_map/ppermute | solution.py:27
  218.7 1.9 collective-permute-start.39
  220.6 1.9 collective-permute-start.36
  222.5 6.0 %collective-permute-start.37 = (f32[1,32]{1,0:T(1,128)S(1)}, f32[1,32]{1,0:T(1,128)S(1)}, u32[]{:S(2)}, u32[]{:S(2)}) collective-permute-start(f32[1,32]{1,0:T(1,128)S(1)} %get-tuple-element.452), channel_id=1, source_target_pairs={{0,64},{64,128},{128,192},{192,256},{256,320},{320,384},{384,448},... | collective-permute-start | bytes 392 | tf_op jit(solution)/shard_map/ppermute | solution.py:26
  230.2 4.0 %collective-permute-start.42 = (f32[16,1]{1,0:T(8,128)S(1)}, f32[16,1]{1,0:T(8,128)S(1)}, u32[]{:S(2)}, u32[]{:S(2)}) collective-permute-start(f32[16,1]{1,0:T(8,128)S(1)} %get-tuple-element.438), channel_id=1, source_target_pairs={{1,0},{2,1},{3,2},{4,3},{5,4},{6,5},{7,6},{8,7},{9,8},{10,9},{11,1... | collective-permute-start | bytes 200 | tf_op jit(solution)/shard_map/ppermute | solution.py:27
  236.1 6.0 %collective-permute-start.41 = (f32[1,64]{1,0:T(1,128)S(1)}, f32[1,64]{1,0:T(1,128)S(1)}, u32[]{:S(2)}, u32[]{:S(2)}) collective-permute-start(f32[1,64]{1,0:T(1,128)S(1)} %get-tuple-element.440), channel_id=1, source_target_pairs={{0,64},{64,128},{128,192},{192,256},{256,320},{320,384},{384,448},... | collective-permute-start | bytes 776 | tf_op jit(solution)/shard_map/ppermute | solution.py:26
  244.1 4.2 %collective-permute-done.43 = f32[16,1]{1,0:T(8,128)S(1)} collective-permute-done((f32[16,1]{1,0:T(8,128)S(1)}, f32[16,1]{1,0:T(8,128)S(1)}, u32[]{:S(2)}, u32[]{:S(2)}) %collective-permute-start.43) | collective-permute-done | bytes 96 | tf_op jit(solution)/shard_map/ppermute | solution.py:26
  252.3 6.0 %collective-permute-start.45 = (f32[1,64]{1,0:T(1,128)S(1)}, f32[1,64]{1,0:T(1,128)S(1)}, u32[]{:S(2)}, u32[]{:S(2)}) collective-permute-start(f32[1,64]{1,0:T(1,128)S(1)} %get-tuple-element.436), channel_id=1, source_target_pairs={{0,64},{64,128},{128,192},{192,256},{256,320},{320,384},{384,448},... | collective-permute-start | bytes 776 | tf_op jit(solution)/shard_map/ppermute | solution.py:26
  260.3 4.2 %collective-permute-done.47 = f32[16,1]{1,0:T(8,128)S(1)} collective-permute-done((f32[16,1]{1,0:T(8,128)S(1)}, f32[16,1]{1,0:T(8,128)S(1)}, u32[]{:S(2)}, u32[]{:S(2)}) %collective-permute-start.47) | collective-permute-done | bytes 96 | tf_op jit(solution)/shard_map/ppermute | solution.py:26
  266.8 6.0 %collective-permute-start.49 = (f32[1,128]{0,1:T(8,128)S(1)}, f32[1,128]{0,1:T(8,128)S(1)}, u32[]{:S(2)}, u32[]{:S(2)}) collective-permute-start(f32[1,128]{0,1:T(8,128)S(1)} %get-tuple-element.424), channel_id=1, source_target_pairs={{0,64},{64,128},{128,192},{192,256},{256,320},{320,384},{384,448},... | collective-permute-start | bytes 1544 | tf_op jit(solution)/shard_map/ppermute | solution.py:26
  274.8 2.4 collective-permute-start.51
  277.8 3.1 %collective-permute-done.51 = f32[32,1]{0,1:T(1,128)S(1)} collective-permute-done((f32[32,1]{0,1:T(1,128)S(1)}, f32[32,1]{0,1:T(1,128)S(1)}, u32[]{:S(2)}, u32[]{:S(2)}) %collective-permute-start.51) | collective-permute-done | bytes 160 | tf_op jit(solution)/shard_map/ppermute | solution.py:26
  283.1 6.0 %collective-permute-start.53 = (f32[1,128]{0,1:T(8,128)S(1)}, f32[1,128]{0,1:T(8,128)S(1)}, u32[]{:S(2)}, u32[]{:S(2)}) collective-permute-start(f32[1,128]{0,1:T(8,128)S(1)} %get-tuple-element.420), channel_id=1, source_target_pairs={{0,64},{64,128},{128,192},{192,256},{256,320},{320,384},{384,448},... | collective-permute-start | bytes 1544 | tf_op jit(solution)/shard_map/ppermute | solution.py:26
  291.1 2.4 collective-permute-start.55
  294.1 3.0 %collective-permute-done.55 = f32[32,1]{0,1:T(1,128)S(1)} collective-permute-done((f32[32,1]{0,1:T(1,128)S(1)}, f32[32,1]{0,1:T(1,128)S(1)}, u32[]{:S(2)}, u32[]{:S(2)}) %collective-permute-start.55) | collective-permute-done | bytes 160 | tf_op jit(solution)/shard_map/ppermute | solution.py:26
  (278 shorter events, 121.4 us)
Async XLA Ops:
  0.6 100.7 %collective-permute-start = (f32[1,128]{0,1:T(8,128)S(1)}, f32[1,128]{0,1:T(8,128)S(1)}, u32[]{:S(2)}, u32[]{:S(2)}) collective-permute-start(f32[1,128]{0,1:T(8,128)S(1)} %broadcast.238), channel_id=1, source_target_pairs={{64,0},{128,64},{192,128},{256,192},{320,256},{384,320},{448,384},... | collective-permute-start | bytes 1544 | tf_op jit(solution)/shard_map/ppermute | solution.py:27
  3.4 98.0 %collective-permute-start.1 = (f32[1,128]{0,1:T(8,128)S(1)}, f32[1,128]{0,1:T(8,128)S(1)}, u32[]{:S(2)}, u32[]{:S(2)}) collective-permute-start(f32[1,128]{0,1:T(8,128)S(1)} %broadcast.238), channel_id=1, source_target_pairs={{0,64},{64,128},{128,192},{192,256},{256,320},{320,384},{384,448},... | collective-permute-start | bytes 1544 | tf_op jit(solution)/shard_map/ppermute | solution.py:26
  8.6 92.7 %collective-permute-start.2 = (f32[32,1]{0,1:T(1,128)S(1)}, f32[32,1]{0,1:T(1,128)S(1)}, u32[]{:S(2)}, u32[]{:S(2)}) collective-permute-start(f32[32,1]{0,1:T(1,128)S(1)} %broadcast.239), channel_id=1, source_target_pairs={{1,0},{2,1},{3,2},{4,3},{5,4},{6,5},{7,6},{8,7},{9,8},{10,9},{11,1... | collective-permute-start | bytes 392 | tf_op jit(solution)/shard_map/ppermute | solution.py:27
  11.6 89.7 %collective-permute-start.3 = (f32[32,1]{0,1:T(1,128)S(1)}, f32[32,1]{0,1:T(1,128)S(1)}, u32[]{:S(2)}, u32[]{:S(2)}) collective-permute-start(f32[32,1]{0,1:T(1,128)S(1)} %broadcast.239), channel_id=1, source_target_pairs={{0,1},{1,2},{2,3},{3,4},{4,5},{5,6},{6,7},{7,8},{8,9},{9,10},{10,1... | collective-permute-start | bytes 392 | tf_op jit(solution)/shard_map/ppermute | solution.py:26
  13.6 132.4 %collective-permute-start.14 = (f32[16,1]{1,0:T(8,128)S(1)}, f32[16,1]{1,0:T(8,128)S(1)}, u32[]{:S(2)}, u32[]{:S(2)}) collective-permute-start(f32[16,1]{1,0:T(8,128)S(1)} %broadcast.242), channel_id=1, source_target_pairs={{1,0},{2,1},{3,2},{4,3},{5,4},{6,5},{7,6},{8,7},{9,8},{10,9},{11,1... | collective-permute-start | bytes 200 | tf_op jit(solution)/shard_map/ppermute | solution.py:27
  91.8 185.4 %all-to-all-start = ((f32[16,1,1]{2,1,0:T(1,128)}), f32[16,1,1]{2,1,0:T(1,128)S(1)}, u32[]{:S(2)}, u32[]{:S(2)}) async-start(f32[16,1,1]{2,1,0:T(1,128)} %bitcast.33), calls=%async_computation | async-start | bytes 16384 | tf_op jit(solution)/shard_map/all_to_all | solution.py:45
  101.6 16.0 %collective-permute-start.4 = (f32[1,128]{0,1:T(8,128)S(1)}, f32[1,128]{0,1:T(8,128)S(1)}, u32[]{:S(2)}, u32[]{:S(2)}) collective-permute-start(f32[1,128]{0,1:T(8,128)S(1)} %get-tuple-element.433), channel_id=1, source_target_pairs={{64,0},{128,64},{192,128},{256,192},{320,256},{384,320},{448,384},... | collective-permute-start | bytes 1544 | tf_op jit(solution)/shard_map/ppermute | solution.py:27
  104.4 13.2 %collective-permute-start.5 = (f32[1,128]{0,1:T(8,128)S(1)}, f32[1,128]{0,1:T(8,128)S(1)}, u32[]{:S(2)}, u32[]{:S(2)}) collective-permute-start(f32[1,128]{0,1:T(8,128)S(1)} %get-tuple-element.432), channel_id=1, source_target_pairs={{0,64},{64,128},{128,192},{192,256},{256,320},{320,384},{384,448},... | collective-permute-start | bytes 1544 | tf_op jit(solution)/shard_map/ppermute | solution.py:26
  117.9 17.9 %collective-permute-start.8 = (f32[1,128]{0,1:T(8,128)S(1)}, f32[1,128]{0,1:T(8,128)S(1)}, u32[]{:S(2)}, u32[]{:S(2)}) collective-permute-start(f32[1,128]{0,1:T(8,128)S(1)} %get-tuple-element.429), channel_id=1, source_target_pairs={{64,0},{128,64},{192,128},{256,192},{320,256},{384,320},{448,384},... | collective-permute-start | bytes 1544 | tf_op jit(solution)/shard_map/ppermute | solution.py:27
  119.9 22.0 %collective-permute-start.9 = (f32[1,128]{0,1:T(8,128)S(1)}, f32[1,128]{0,1:T(8,128)S(1)}, u32[]{:S(2)}, u32[]{:S(2)}) collective-permute-start(f32[1,128]{0,1:T(8,128)S(1)} %get-tuple-element.428), channel_id=1, source_target_pairs={{0,64},{64,128},{128,192},{192,256},{256,320},{320,384},{384,448},... | collective-permute-start | bytes 1544 | tf_op jit(solution)/shard_map/ppermute | solution.py:26
  130.3 15.8 %collective-permute-start.15 = (f32[16,1]{1,0:T(8,128)S(1)}, f32[16,1]{1,0:T(8,128)S(1)}, u32[]{:S(2)}, u32[]{:S(2)}) collective-permute-start(f32[16,1]{1,0:T(8,128)S(1)} %broadcast.242), channel_id=1, source_target_pairs={{0,1},{1,2},{2,3},{3,4},{4,5},{5,6},{6,7},{7,8},{8,9},{9,10},{10,1... | collective-permute-start | bytes 200 | tf_op jit(solution)/shard_map/ppermute | solution.py:26
  133.9 12.1 %collective-permute-start.12 = (f32[1,64]{1,0:T(1,128)S(1)}, f32[1,64]{1,0:T(1,128)S(1)}, u32[]{:S(2)}, u32[]{:S(2)}) collective-permute-start(f32[1,64]{1,0:T(1,128)S(1)} %broadcast.241), channel_id=1, source_target_pairs={{64,0},{128,64},{192,128},{256,192},{320,256},{384,320},{448,384},... | collective-permute-start | bytes 776 | tf_op jit(solution)/shard_map/ppermute | solution.py:27
  135.9 10.2 %collective-permute-start.13 = (f32[1,64]{1,0:T(1,128)S(1)}, f32[1,64]{1,0:T(1,128)S(1)}, u32[]{:S(2)}, u32[]{:S(2)}) collective-permute-start(f32[1,64]{1,0:T(1,128)S(1)} %broadcast.241), channel_id=1, source_target_pairs={{0,64},{64,128},{128,192},{192,256},{256,320},{320,384},{384,448},... | collective-permute-start | bytes 776 | tf_op jit(solution)/shard_map/ppermute | solution.py:26
  141.9 42.1 %collective-permute-start.26 = (f32[8,1]{1,0:T(8,128)S(1)}, f32[8,1]{1,0:T(8,128)S(1)}, u32[]{:S(2)}, u32[]{:S(2)}) collective-permute-start(f32[8,1]{1,0:T(8,128)S(1)} %broadcast.246), channel_id=1, source_target_pairs={{1,0},{2,1},{3,2},{4,3},{5,4},{6,5},{7,6},{8,7},{9,8},{10,9},{11,1... | collective-permute-start | bytes 104 | tf_op jit(solution)/shard_map/ppermute | solution.py:27
  146.2 12.4 %collective-permute-start.18 = (f32[16,1]{1,0:T(8,128)S(1)}, f32[16,1]{1,0:T(8,128)S(1)}, u32[]{:S(2)}, u32[]{:S(2)}) collective-permute-start(f32[16,1]{1,0:T(8,128)S(1)} %get-tuple-element.446), channel_id=1, source_target_pairs={{1,0},{2,1},{3,2},{4,3},{5,4},{6,5},{7,6},{8,7},{9,8},{10,9},{11,1... | collective-permute-start | bytes 200 | tf_op jit(solution)/shard_map/ppermute | solution.py:27
  148.7 14.2 %collective-permute-start.16 = (f32[1,64]{1,0:T(1,128)S(1)}, f32[1,64]{1,0:T(1,128)S(1)}, u32[]{:S(2)}, u32[]{:S(2)}) collective-permute-start(f32[1,64]{1,0:T(1,128)S(1)} %get-tuple-element.449), channel_id=1, source_target_pairs={{64,0},{128,64},{192,128},{256,192},{320,256},{384,320},{448,384},... | collective-permute-start | bytes 776 | tf_op jit(solution)/shard_map/ppermute | solution.py:27
  150.6 12.2 %collective-permute-start.17 = (f32[1,64]{1,0:T(1,128)S(1)}, f32[1,64]{1,0:T(1,128)S(1)}, u32[]{:S(2)}, u32[]{:S(2)}) collective-permute-start(f32[1,64]{1,0:T(1,128)S(1)} %get-tuple-element.448), channel_id=1, source_target_pairs={{0,64},{64,128},{128,192},{192,256},{256,320},{320,384},{384,448},... | collective-permute-start | bytes 776 | tf_op jit(solution)/shard_map/ppermute | solution.py:26
  156.7 6.2 %collective-permute-start.19 = (f32[16,1]{1,0:T(8,128)S(1)}, f32[16,1]{1,0:T(8,128)S(1)}, u32[]{:S(2)}, u32[]{:S(2)}) collective-permute-start(f32[16,1]{1,0:T(8,128)S(1)} %get-tuple-element.447), channel_id=1, source_target_pairs={{0,1},{1,2},{2,3},{3,4},{4,5},{5,6},{6,7},{7,8},{8,9},{9,10},{10,1... | collective-permute-start | bytes 200 | tf_op jit(solution)/shard_map/ppermute | solution.py:26
  158.6 25.4 %collective-permute-start.27 = (f32[8,1]{1,0:T(8,128)S(1)}, f32[8,1]{1,0:T(8,128)S(1)}, u32[]{:S(2)}, u32[]{:S(2)}) collective-permute-start(f32[8,1]{1,0:T(8,128)S(1)} %broadcast.246), channel_id=1, source_target_pairs={{0,1},{1,2},{2,3},{3,4},{4,5},{5,6},{6,7},{7,8},{8,9},{9,10},{10,1... | collective-permute-start | bytes 104 | tf_op jit(solution)/shard_map/ppermute | solution.py:26
  163.0 6.4 %collective-permute-start.22 = (f32[16,1]{1,0:T(8,128)S(1)}, f32[16,1]{1,0:T(8,128)S(1)}, u32[]{:S(2)}, u32[]{:S(2)}) collective-permute-start(f32[16,1]{1,0:T(8,128)S(1)} %get-tuple-element.442), channel_id=1, source_target_pairs={{1,0},{2,1},{3,2},{4,3},{5,4},{6,5},{7,6},{8,7},{9,8},{10,9},{11,1... | collective-permute-start | bytes 200 | tf_op jit(solution)/shard_map/ppermute | solution.py:27
  165.6 9.9 %collective-permute-start.23 = (f32[16,1]{1,0:T(8,128)S(1)}, f32[16,1]{1,0:T(8,128)S(1)}, u32[]{:S(2)}, u32[]{:S(2)}) collective-permute-start(f32[16,1]{1,0:T(8,128)S(1)} %get-tuple-element.443), channel_id=1, source_target_pairs={{0,1},{1,2},{2,3},{3,4},{4,5},{5,6},{6,7},{7,8},{8,9},{9,10},{10,1... | collective-permute-start | bytes 200 | tf_op jit(solution)/shard_map/ppermute | solution.py:26
  167.5 9.9 %collective-permute-start.20 = (f32[1,64]{1,0:T(1,128)S(1)}, f32[1,64]{1,0:T(1,128)S(1)}, u32[]{:S(2)}, u32[]{:S(2)}) collective-permute-start(f32[1,64]{1,0:T(1,128)S(1)} %get-tuple-element.445), channel_id=1, source_target_pairs={{64,0},{128,64},{192,128},{256,192},{320,256},{384,320},{448,384},... | collective-permute-start | bytes 776 | tf_op jit(solution)/shard_map/ppermute | solution.py:27
  169.5 14.0 %collective-permute-start.21 = (f32[1,64]{1,0:T(1,128)S(1)}, f32[1,64]{1,0:T(1,128)S(1)}, u32[]{:S(2)}, u32[]{:S(2)}) collective-permute-start(f32[1,64]{1,0:T(1,128)S(1)} %get-tuple-element.444), channel_id=1, source_target_pairs={{0,64},{64,128},{128,192},{192,256},{256,320},{320,384},{384,448},... | collective-permute-start | bytes 776 | tf_op jit(solution)/shard_map/ppermute | solution.py:26
  175.5 8.5 %collective-permute-start.24 = (f32[1,32]{1,0:T(1,128)S(1)}, f32[1,32]{1,0:T(1,128)S(1)}, u32[]{:S(2)}, u32[]{:S(2)}) collective-permute-start(f32[1,32]{1,0:T(1,128)S(1)} %broadcast.245), channel_id=1, source_target_pairs={{64,0},{128,64},{192,128},{256,192},{320,256},{384,320},{448,384},... | collective-permute-start | bytes 392 | tf_op jit(solution)/shard_map/ppermute | solution.py:27
  177.5 7.3 %collective-permute-start.25 = (f32[1,32]{1,0:T(1,128)S(1)}, f32[1,32]{1,0:T(1,128)S(1)}, u32[]{:S(2)}, u32[]{:S(2)}) collective-permute-start(f32[1,32]{1,0:T(1,128)S(1)} %broadcast.245), channel_id=1, source_target_pairs={{0,64},{64,128},{128,192},{192,256},{256,320},{320,384},{384,448},... | collective-permute-start | bytes 392 | tf_op jit(solution)/shard_map/ppermute | solution.py:26
  184.9 13.1 %collective-permute-start.30 = (f32[8,1]{1,0:T(8,128)S(1)}, f32[8,1]{1,0:T(8,128)S(1)}, u32[]{:S(2)}, u32[]{:S(2)}) collective-permute-start(f32[8,1]{1,0:T(8,128)S(1)} %get-tuple-element.458), channel_id=1, source_target_pairs={{1,0},{2,1},{3,2},{4,3},{5,4},{6,5},{7,6},{8,7},{9,8},{10,9},{11,1... | collective-permute-start | bytes 104 | tf_op jit(solution)/shard_map/ppermute | solution.py:27
  188.1 9.9 %collective-permute-start.31 = (f32[8,1]{1,0:T(8,128)S(1)}, f32[8,1]{1,0:T(8,128)S(1)}, u32[]{:S(2)}, u32[]{:S(2)}) collective-permute-start(f32[8,1]{1,0:T(8,128)S(1)} %get-tuple-element.459), channel_id=1, source_target_pairs={{0,1},{1,2},{2,3},{3,4},{4,5},{5,6},{6,7},{7,8},{8,9},{9,10},{10,1... | collective-permute-start | bytes 104 | tf_op jit(solution)/shard_map/ppermute | solution.py:26
  190.0 8.0 %collective-permute-start.28 = (f32[1,32]{1,0:T(1,128)S(1)}, f32[1,32]{1,0:T(1,128)S(1)}, u32[]{:S(2)}, u32[]{:S(2)}) collective-permute-start(f32[1,32]{1,0:T(1,128)S(1)} %get-tuple-element.461), channel_id=1, source_target_pairs={{64,0},{128,64},{192,128},{256,192},{320,256},{384,320},{448,384},... | collective-permute-start | bytes 392 | tf_op jit(solution)/shard_map/ppermute | solution.py:27
  191.9 7.3 %collective-permute-start.29 = (f32[1,32]{1,0:T(1,128)S(1)}, f32[1,32]{1,0:T(1,128)S(1)}, u32[]{:S(2)}, u32[]{:S(2)}) collective-permute-start(f32[1,32]{1,0:T(1,128)S(1)} %get-tuple-element.460), channel_id=1, source_target_pairs={{0,64},{64,128},{128,192},{192,256},{256,320},{320,384},{384,448},... | collective-permute-start | bytes 392 | tf_op jit(solution)/shard_map/ppermute | solution.py:26
  199.4 13.9 %collective-permute-start.34 = (f32[8,1]{1,0:T(8,128)S(1)}, f32[8,1]{1,0:T(8,128)S(1)}, u32[]{:S(2)}, u32[]{:S(2)}) collective-permute-start(f32[8,1]{1,0:T(8,128)S(1)} %get-tuple-element.454), channel_id=1, source_target_pairs={{1,0},{2,1},{3,2},{4,3},{5,4},{6,5},{7,6},{8,7},{9,8},{10,9},{11,1... | collective-permute-start | bytes 104 | tf_op jit(solution)/shard_map/ppermute | solution.py:27
  203.4 9.9 %collective-permute-start.35 = (f32[8,1]{1,0:T(8,128)S(1)}, f32[8,1]{1,0:T(8,128)S(1)}, u32[]{:S(2)}, u32[]{:S(2)}) collective-permute-start(f32[8,1]{1,0:T(8,128)S(1)} %get-tuple-element.455), channel_id=1, source_target_pairs={{0,1},{1,2},{2,3},{3,4},{4,5},{5,6},{6,7},{7,8},{8,9},{9,10},{10,1... | collective-permute-start | bytes 104 | tf_op jit(solution)/shard_map/ppermute | solution.py:26
  205.3 8.0 %collective-permute-start.32 = (f32[1,32]{1,0:T(1,128)S(1)}, f32[1,32]{1,0:T(1,128)S(1)}, u32[]{:S(2)}, u32[]{:S(2)}) collective-permute-start(f32[1,32]{1,0:T(1,128)S(1)} %get-tuple-element.457), channel_id=1, source_target_pairs={{64,0},{128,64},{192,128},{256,192},{320,256},{384,320},{448,384},... | collective-permute-start | bytes 392 | tf_op jit(solution)/shard_map/ppermute | solution.py:27
  207.2 7.3 %collective-permute-start.33 = (f32[1,32]{1,0:T(1,128)S(1)}, f32[1,32]{1,0:T(1,128)S(1)}, u32[]{:S(2)}, u32[]{:S(2)}) collective-permute-start(f32[1,32]{1,0:T(1,128)S(1)} %get-tuple-element.456), channel_id=1, source_target_pairs={{0,64},{64,128},{128,192},{192,256},{256,320},{320,384},{384,448},... | collective-permute-start | bytes 392 | tf_op jit(solution)/shard_map/ppermute | solution.py:26
  214.7 13.9 %collective-permute-start.38 = (f32[8,1]{1,0:T(8,128)S(1)}, f32[8,1]{1,0:T(8,128)S(1)}, u32[]{:S(2)}, u32[]{:S(2)}) collective-permute-start(f32[8,1]{1,0:T(8,128)S(1)} %get-tuple-element.450), channel_id=1, source_target_pairs={{1,0},{2,1},{3,2},{4,3},{5,4},{6,5},{7,6},{8,7},{9,8},{10,9},{11,1... | collective-permute-start | bytes 104 | tf_op jit(solution)/shard_map/ppermute | solution.py:27
  218.7 9.9 %collective-permute-start.39 = (f32[8,1]{1,0:T(8,128)S(1)}, f32[8,1]{1,0:T(8,128)S(1)}, u32[]{:S(2)}, u32[]{:S(2)}) collective-permute-start(f32[8,1]{1,0:T(8,128)S(1)} %get-tuple-element.451), channel_id=1, source_target_pairs={{0,1},{1,2},{2,3},{3,4},{4,5},{5,6},{6,7},{7,8},{8,9},{9,10},{10,1... | collective-permute-start | bytes 104 | tf_op jit(solution)/shard_map/ppermute | solution.py:26
  220.6 8.0 %collective-permute-start.36 = (f32[1,32]{1,0:T(1,128)S(1)}, f32[1,32]{1,0:T(1,128)S(1)}, u32[]{:S(2)}, u32[]{:S(2)}) collective-permute-start(f32[1,32]{1,0:T(1,128)S(1)} %get-tuple-element.453), channel_id=1, source_target_pairs={{64,0},{128,64},{192,128},{256,192},{320,256},{384,320},{448,384},... | collective-permute-start | bytes 392 | tf_op jit(solution)/shard_map/ppermute | solution.py:27
  222.5 7.3 %collective-permute-start.37 = (f32[1,32]{1,0:T(1,128)S(1)}, f32[1,32]{1,0:T(1,128)S(1)}, u32[]{:S(2)}, u32[]{:S(2)}) collective-permute-start(f32[1,32]{1,0:T(1,128)S(1)} %get-tuple-element.452), channel_id=1, source_target_pairs={{0,64},{64,128},{128,192},{192,256},{256,320},{320,384},{384,448},... | collective-permute-start | bytes 392 | tf_op jit(solution)/shard_map/ppermute | solution.py:26
  230.2 13.9 %collective-permute-start.42 = (f32[16,1]{1,0:T(8,128)S(1)}, f32[16,1]{1,0:T(8,128)S(1)}, u32[]{:S(2)}, u32[]{:S(2)}) collective-permute-start(f32[16,1]{1,0:T(8,128)S(1)} %get-tuple-element.438), channel_id=1, source_target_pairs={{1,0},{2,1},{3,2},{4,3},{5,4},{6,5},{7,6},{8,7},{9,8},{10,9},{11,1... | collective-permute-start | bytes 200 | tf_op jit(solution)/shard_map/ppermute | solution.py:27
  234.1 14.2 %collective-permute-start.40 = (f32[1,64]{1,0:T(1,128)S(1)}, f32[1,64]{1,0:T(1,128)S(1)}, u32[]{:S(2)}, u32[]{:S(2)}) collective-permute-start(f32[1,64]{1,0:T(1,128)S(1)} %get-tuple-element.441), channel_id=1, source_target_pairs={{64,0},{128,64},{192,128},{256,192},{320,256},{384,320},{448,384},... | collective-permute-start | bytes 776 | tf_op jit(solution)/shard_map/ppermute | solution.py:27
  236.1 12.2 %collective-permute-start.41 = (f32[1,64]{1,0:T(1,128)S(1)}, f32[1,64]{1,0:T(1,128)S(1)}, u32[]{:S(2)}, u32[]{:S(2)}) collective-permute-start(f32[1,64]{1,0:T(1,128)S(1)} %get-tuple-element.440), channel_id=1, source_target_pairs={{0,64},{64,128},{128,192},{192,256},{256,320},{320,384},{384,448},... | collective-permute-start | bytes 776 | tf_op jit(solution)/shard_map/ppermute | solution.py:26
  242.1 6.2 %collective-permute-start.43 = (f32[16,1]{1,0:T(8,128)S(1)}, f32[16,1]{1,0:T(8,128)S(1)}, u32[]{:S(2)}, u32[]{:S(2)}) collective-permute-start(f32[16,1]{1,0:T(8,128)S(1)} %get-tuple-element.439), channel_id=1, source_target_pairs={{0,1},{1,2},{2,3},{3,4},{4,5},{5,6},{6,7},{7,8},{8,9},{9,10},{10,1... | collective-permute-start | bytes 200 | tf_op jit(solution)/shard_map/ppermute | solution.py:26
  248.5 11.8 %collective-permute-start.46 = (f32[16,1]{1,0:T(8,128)S(1)}, f32[16,1]{1,0:T(8,128)S(1)}, u32[]{:S(2)}, u32[]{:S(2)}) collective-permute-start(f32[16,1]{1,0:T(8,128)S(1)} %get-tuple-element.434), channel_id=1, source_target_pairs={{1,0},{2,1},{3,2},{4,3},{5,4},{6,5},{7,6},{8,7},{9,8},{10,9},{11,1... | collective-permute-start | bytes 200 | tf_op jit(solution)/shard_map/ppermute | solution.py:27
  250.4 14.2 %collective-permute-start.44 = (f32[1,64]{1,0:T(1,128)S(1)}, f32[1,64]{1,0:T(1,128)S(1)}, u32[]{:S(2)}, u32[]{:S(2)}) collective-permute-start(f32[1,64]{1,0:T(1,128)S(1)} %get-tuple-element.437), channel_id=1, source_target_pairs={{64,0},{128,64},{192,128},{256,192},{320,256},{384,320},{448,384},... | collective-permute-start | bytes 776 | tf_op jit(solution)/shard_map/ppermute | solution.py:27
  252.3 12.2 %collective-permute-start.45 = (f32[1,64]{1,0:T(1,128)S(1)}, f32[1,64]{1,0:T(1,128)S(1)}, u32[]{:S(2)}, u32[]{:S(2)}) collective-permute-start(f32[1,64]{1,0:T(1,128)S(1)} %get-tuple-element.436), channel_id=1, source_target_pairs={{0,64},{64,128},{128,192},{192,256},{256,320},{320,384},{384,448},... | collective-permute-start | bytes 776 | tf_op jit(solution)/shard_map/ppermute | solution.py:26
  264.9 16.0 %collective-permute-start.48 = (f32[1,128]{0,1:T(8,128)S(1)}, f32[1,128]{0,1:T(8,128)S(1)}, u32[]{:S(2)}, u32[]{:S(2)}) collective-permute-start(f32[1,128]{0,1:T(8,128)S(1)} %get-tuple-element.425), channel_id=1, source_target_pairs={{64,0},{128,64},{192,128},{256,192},{320,256},{384,320},{448,384},... | collective-permute-start | bytes 1544 | tf_op jit(solution)/shard_map/ppermute | solution.py:27
  266.8 14.1 %collective-permute-start.49 = (f32[1,128]{0,1:T(8,128)S(1)}, f32[1,128]{0,1:T(8,128)S(1)}, u32[]{:S(2)}, u32[]{:S(2)}) collective-permute-start(f32[1,128]{0,1:T(8,128)S(1)} %get-tuple-element.424), channel_id=1, source_target_pairs={{0,64},{64,128},{128,192},{192,256},{256,320},{320,384},{384,448},... | collective-permute-start | bytes 1544 | tf_op jit(solution)/shard_map/ppermute | solution.py:26
  281.2 16.0 %collective-permute-start.52 = (f32[1,128]{0,1:T(8,128)S(1)}, f32[1,128]{0,1:T(8,128)S(1)}, u32[]{:S(2)}, u32[]{:S(2)}) collective-permute-start(f32[1,128]{0,1:T(8,128)S(1)} %get-tuple-element.421), channel_id=1, source_target_pairs={{64,0},{128,64},{192,128},{256,192},{320,256},{384,320},{448,384},... | collective-permute-start | bytes 1544 | tf_op jit(solution)/shard_map/ppermute | solution.py:27
  283.1 14.1 %collective-permute-start.53 = (f32[1,128]{0,1:T(8,128)S(1)}, f32[1,128]{0,1:T(8,128)S(1)}, u32[]{:S(2)}, u32[]{:S(2)}) collective-permute-start(f32[1,128]{0,1:T(8,128)S(1)} %get-tuple-element.420), channel_id=1, source_target_pairs={{0,64},{64,128},{128,192},{192,256},{256,320},{320,384},{384,448},... | collective-permute-start | bytes 1544 | tf_op jit(solution)/shard_map/ppermute | solution.py:26
  (16 other events, 71.5 us)
where the time goes:
time: 301 us; the launch traced here: 299 us
  starting transfers between devices  188 us (62%)
  matrix products  54.8 us (18%)
  waiting for transfers between devices  25 us (8%)
  local copies, waits for them, and re-layouts  14.8 us (5%)
  other arithmetic  9.66 us (3%)
  between operations  6.14 us (2%)
    ppermute x28, starting transfers between devices, with_halo(): lax.ppermute(last, axis, up)  113 us
    ppermute x28, starting transfers between devices, with_halo(): lax.ppermute(leading, axis, [(b, a) for a, b in up])  68.6 us
    ppermute x28, waiting for transfers between devices, with_halo(): lax.ppermute(last, axis, up)  24.9 us
    dot_general x16, matrix products, advance(): jnp.einsum('rs,sbc->rbc', consumed_weighting, spec_part, precision=high)  22.2 us
    dot_general x16, matrix products, advance(): change = jnp.einsum('rs,rbc->sbc', molar_coefficient, flux, precision=high)  17.3 us
    dot_general x16, matrix products, advance(): release = jnp.einsum('r,rbc->bc', enthalpy_released, flux, precision=high)  14.4 us
    all_to_all x1, starting transfers between devices, sent_and_summed(): pieces = lax.all_to_all(split_up(shard, dim, size), axis, 0, 0, tiled=True)  7.17 us
  transfers between devices with their start and end apart: 57, of which 11 were waited for; matrix products, arithmetic and copies ran while one was open for 26% of the time, Pallas kernels for 0%

commit v1 on v0

v1 whole, which is shorter than its diff:
```python
import functools

import jax
import jax.numpy as jnp
from jax import lax
from jax.experimental import pallas as pl
from jax.experimental.pallas import tpu as pltpu
from jax.sharding import PartitionSpec as P

NS = 53
NR = 325
MAXSUB = 4
TILES = 16
ROWS = 32
LANES = 128
STATE = 64
REACT = 336
TEMP_ROW = 53
HEAT_ROW = 54
GROUPS = 4
GROUP_ROWS = ROWS // GROUPS
step_time = 0.4
MESH = pl.DeviceIdType.MESH


def halves(x):
    top = x.astype(jnp.bfloat16)
    rest = (x - top.astype(jnp.float32)).astype(jnp.bfloat16)
    return top, rest


def chemistry_kernel(
    counts,
    owners,
    chem_hbm,
    temp_ref,
    flow_ref,
    weight_ref,
    molar_ref,
    factor_ref,
    energy_ref,
    release_ref,
    chem_out,
    temp_out,
    rhs_ref,
    share_ref,
    chem_buf,
    out_buf,
    state,
    wide,
    energy_cols,
    first,
    second,
    third,
    pad,
    in_sem,
    out_sem,
):
    def fetch(g):
        return pltpu.make_async_copy(
            chem_hbm.at[:, pl.ds(g * GROUP_ROWS, GROUP_ROWS), :], chem_buf.at[g], in_sem.at[g]
        )

    def emit(g):
        return pltpu.make_async_copy(
            out_buf.at[g], chem_out.at[:, pl.ds(g * GROUP_ROWS, GROUP_ROWS), :], out_sem.at[g]
        )

    for g in range(GROUPS):
        fetch(g).start()

    wide[...] = jnp.zeros_like(wide)
    wide[0:NS, 0:NR] = weight_ref[...] * jnp.exp(factor_ref[...].reshape(1, NR))
    whole = wide[0:STATE, :]
    top = whole.astype(jnp.bfloat16).astype(jnp.float32)
    both = jnp.concatenate([top, whole - top], axis=0).T[0:REACT].astype(jnp.bfloat16)
    first[:, 0:128] = both
    first[:, 128:256] = both

    pad[...] = jnp.zeros_like(pad)
    pad[0:1, 0:NR] = energy_ref[...].reshape(1, NR) * -1.4426950408889634
    columns = jnp.broadcast_to(pad[...], (LANES, 384)).T[0:REACT]
    energy_cols[:, 0:128] = columns
    energy_cols[:, 128:256] = columns

    wide[0:NS, 0:NR] = molar_ref[...]
    wide[TEMP_ROW : TEMP_ROW + 1, 0:NR] = release_ref[...].reshape(1, NR)
    wide[HEAT_ROW : HEAT_ROW + 1, 0:NR] = release_ref[...].reshape(1, NR)
    whole = wide[0:56, :]
    top = whole.astype(jnp.bfloat16).astype(jnp.float32)
    hi = jnp.concatenate([top, whole - top], axis=0).astype(jnp.bfloat16)
    second[:, 0:384] = hi
    third[...] = wide[...].astype(jnp.bfloat16)

    for g in range(GROUPS):
        fetch(g).wait()
        rows = chem_buf.at[g].reshape(NS * GROUP_ROWS, LANES)
        for j in range(GROUP_ROWS):
            r = g * GROUP_ROWS + j
            lanes = pl.ds(r * LANES, LANES)
            state[0:NS, lanes] = rows[pl.ds(j, NS, stride=GROUP_ROWS), :]
    state[NS:STATE, :] = jnp.zeros((STATE - NS, ROWS * LANES), jnp.float32)
    for r in range(ROWS):
        state[TEMP_ROW : TEMP_ROW + 1, r * LANES : (r + 1) * LANES] = temp_ref[r : r + 1, :]

    def turn_body(turn, carry):
        def before(t):
            now = state[:, t * 256 : (t + 1) * 256]
            top, rest = halves(now)
            taken = jnp.concatenate([top, top, rest, rest], axis=0)
            return jnp.dot(first[...], taken, preferred_element_type=jnp.float32)

        def after(t, progress):
            cells = pl.ds(t * 256, 256)
            inverse = 1.0 / (1.0 + jnp.abs(state[TEMP_ROW : TEMP_ROW + 1, cells]))
            flux = jnp.exp2(energy_cols[...] * inverse) * progress
            top, rest = halves(flux)
            made = jnp.dot(second[:, 0:REACT], top, preferred_element_type=jnp.float32)
            more = jnp.dot(third[:, 0:REACT], rest, preferred_element_type=jnp.float32)
            change = made[0:56] + made[56:112] + more[0:56]
            count = jnp.full((1, 256), counts[0, t], jnp.int32)
            width = step_time / count.astype(jnp.float32)
            delta = jnp.where(turn < count, width, 0.0)
            state[0:56, cells] += delta * change

        ahead = before(0)
        for t in range(TILES):
            progress = ahead
            if t + 1 < TILES:
                ahead = before(t + 1)
            after(t, progress)
        return carry

    lax.fori_loop(0, MAXSUB, turn_body, 0)

    for g in range(GROUPS):
        rows = out_buf.at[g].reshape(NS * GROUP_ROWS, LANES)
        for j in range(GROUP_ROWS):
            r = g * GROUP_ROWS + j
            rows[pl.ds(j, NS, stride=GROUP_ROWS), :] = state[0:NS, pl.ds(r * LANES, LANES)]
        emit(g).start()
    place = lax.broadcasted_iota(jnp.int32, (TILES, LANES), 0)
    shares = jnp.zeros((TILES, LANES), jnp.float32)
    for r in range(ROWS):
        lanes = slice(r * LANES, (r + 1) * LANES)
        heat = state[HEAT_ROW : HEAT_ROW + 1, lanes]
        temp_out[r : r + 1, :] = state[TEMP_ROW : TEMP_ROW + 1, lanes]
        rhs_ref[r : r + 1, :] = flow_ref[r : r + 1, :] + heat
        shares += jnp.where(place == owners[0, r // 2], heat * heat, 0.0)
    for o in range(TILES):
        share_ref[o] = shares[o : o + 1, :]
    for g in range(GROUPS):
        emit(g).wait()


def chemistry(chem, temp, flow, counts, owners, weight, molar, factor, energy, release):
    vmem = pl.BlockSpec(memory_space=pltpu.VMEM)
    smem = pl.BlockSpec(memory_space=pltpu.SMEM)
    hbm = pl.BlockSpec(memory_space=pl.ANY)
    f32 = jnp.float32
    return pl.pallas_call(
        chemistry_kernel,
        name="chemistry",
        out_shape=(
            jax.ShapeDtypeStruct((NS, ROWS, LANES), f32),
            jax.ShapeDtypeStruct((ROWS, LANES), f32),
            jax.ShapeDtypeStruct((ROWS, LANES), f32),
            jax.ShapeDtypeStruct((TILES, 1, LANES), f32),
        ),
        in_specs=[smem, smem, hbm, vmem, vmem, vmem, vmem, vmem, vmem, vmem],
        out_specs=(hbm, vmem, vmem, vmem),
        scratch_shapes=[
            pltpu.VMEM((GROUPS, NS, GROUP_ROWS, LANES), f32),
            pltpu.VMEM((GROUPS, NS, GROUP_ROWS, LANES), f32),
            pltpu.VMEM((STATE, ROWS * LANES), f32),
            pltpu.VMEM((STATE, 384), f32),
            pltpu.VMEM((REACT, 256), f32),
            pltpu.VMEM((REACT, 256), jnp.bfloat16),
            pltpu.VMEM((112, 384), jnp.bfloat16),
            pltpu.VMEM((STATE, 384), jnp.bfloat16),
            pltpu.VMEM((1, 384), f32),
            pltpu.SemaphoreType.DMA((GROUPS,)),
            pltpu.SemaphoreType.DMA((GROUPS,)),
        ],
    )(
        counts,
        owners,
        chem,
        temp,
        flow,
        weight.T,
        molar.T,
        factor,
        energy,
        release,
    )


SIDES = tuple((a, b) for a in (-1, 0, 1) for b in (-1, 0, 1) if (a, b) != (0, 0))


def shifted(x, by, axis):
    return pltpu.roll(x, by % x.shape[axis], axis)


def beside(u, d):
    return (shifted(u, d, 0) + shifted(u, -d, 0)) + (shifted(u, d, 1) + shifted(u, -d, 1))


def pooled(x, d, row_first, lane_first):
    x = x + jnp.where(row_first, shifted(x, -d, 0), shifted(x, d, 0))
    return x + jnp.where(lane_first, shifted(x, -d, 1), shifted(x, d, 1))


def projection(rhs, inside):
    rows = lax.broadcasted_iota(jnp.int32, rhs.shape, 0)
    lanes = lax.broadcasted_iota(jnp.int32, rhs.shape, 1)
    weigh = jnp.where(inside, 0.2, 0.0)

    def sweep(u, f, d):
        return 0.2 * u + weigh * (f + beside(u, d))

    f0 = rhs
    u0 = sweep(weigh * f0, f0, 1)
    r0 = f0 - (4.0 * u0 - beside(u0, 1))
    f1 = pooled(r0, 1, (rows & 1) == 0, (lanes & 1) == 0)
    u1 = sweep(weigh * f1, f1, 2)
    r1 = f1 - (4.0 * u1 - beside(u1, 2))
    f2 = pooled(r1, 2, (rows & 2) == 0, (lanes & 2) == 0)
    u2 = weigh * f2
    for _ in range(3):
        u2 = sweep(u2, f2, 4)
    u1 = u1 + u2
    for _ in range(2):
        u1 = sweep(u1, f1, 2)
    u0 = u0 + u1
    for _ in range(2):
        u0 = sweep(u0, f0, 1)
    return u0


def project_kernel(
    gx, gy, rhs_ref, share_ref, field_ref, burden_ref, around, parts, send, recv, part_send, part_recv
):
    i = lax.axis_index("gx")
    j = lax.axis_index("gy")

    def there(a, b):
        here = [i + a >= 0] if a < 0 else [i + a < gx] if a > 0 else []
        here += [j + b >= 0] if b < 0 else [j + b < gy] if b > 0 else []
        return functools.reduce(jnp.logical_and, here)

    def halo(n):
        a, b = SIDES[n]
        return pltpu.make_async_remote_copy(
            src_ref=rhs_ref,
            dst_ref=around.at[len(SIDES) - 1 - n],
            send_sem=send.at[n],
            recv_sem=recv.at[len(SIDES) - 1 - n],
            device_id={"gx": i + a, "gy": j + b},
            device_id_type=MESH,
        )

    def part(d):
        peer = lax.rem(i + d, gx)
        return pltpu.make_async_remote_copy(
            src_ref=share_ref.at[peer],
            dst_ref=parts.at[d],
            send_sem=part_send.at[d],
            recv_sem=part_recv.at[d],
            device_id={"gx": peer, "gy": j},
            device_id_type=MESH,
        )

    barrier = pltpu.get_barrier_semaphore()
    expected = jnp.int32(gx - 1)
    for d in range(1, gx):
        pl.semaphore_signal(
            barrier, inc=1, device_id={"gx": lax.rem(i + d, gx), "gy": j}, device_id_type=MESH
        )
    for a, b in SIDES:
        if b == 0:
            continue
        expected += there(a, b).astype(jnp.int32)

        @pl.when(there(a, b))
        def _(a=a, b=b):
            pl.semaphore_signal(
                barrier, inc=1, device_id={"gx": i + a, "gy": j + b}, device_id_type=MESH
            )

    pl.semaphore_wait(barrier, expected)

    for n, (a, b) in enumerate(SIDES):

        @pl.when(there(a, b))
        def _(n=n):
            halo(n).start()

    for d in range(1, gx):
        part(d).start()

    for n, (a, b) in enumerate(SIDES):
        @pl.when(there(a, b))
        def _(n=n, a=a, b=b):
            pltpu.make_async_remote_copy(
                src_ref=rhs_ref,
                dst_ref=around.at[n],
                send_sem=send.at[n],
                recv_sem=recv.at[n],
                device_id={"gx": i + a, "gy": j + b},
                device_id_type=MESH,
            ).wait_recv()

    blocks = {side: around[n] for n, side in enumerate(SIDES)}
    blocks[(0, 0)] = rhs_ref[...]
    west, middle, east = (
        pltpu.roll(jnp.concatenate([blocks[(a, b)] for a in (-1, 0, 1)], axis=0), 64, 1)
        for b in (-1, 0, 1)
    )
    lane = lax.broadcasted_iota(jnp.int32, west.shape, 1)
    grid = jnp.concatenate(
        [jnp.where(lane < 64, west, middle), jnp.where(lane < 64, middle, east)], axis=1
    )
    rows = lax.broadcasted_iota(jnp.int32, grid.shape, 0) + (i - 1) * ROWS
    lanes = lax.broadcasted_iota(jnp.int32, grid.shape, 1) + (j * LANES - 64)
    inside = (rows >= 0) & (rows < gx * ROWS) & (lanes >= 0) & (lanes < gy * LANES)
    field = projection(jnp.where(inside, grid, 0.0), inside)[ROWS : 2 * ROWS]
    left, right = pltpu.roll(field[:, 0:128], 64, 1), pltpu.roll(field[:, 128:256], 64, 1)
    lane = lax.broadcasted_iota(jnp.int32, left.shape, 1)
    field_ref[...] = jnp.where(lane < 64, left, right)

    total = share_ref[i]
    for d in range(1, gx):
        part(d).wait_recv()
        total = total + parts[d]
    burden_ref[...] = jnp.sum(total, axis=1, keepdims=True) / float(ROWS * LANES)

    for n, (a, b) in enumerate(SIDES):

        @pl.when(there(a, b))
        def _(n=n):
            halo(n).wait_send()

    for d in range(1, gx):
        part(d).wait_send()


def project(rhs, shares, gx, gy):
    vmem = pl.BlockSpec(memory_space=pltpu.VMEM)
    f32 = jnp.float32
    return pl.pallas_call(
        functools.partial(project_kernel, gx, gy),
        name="project",
        out_shape=(
            jax.ShapeDtypeStruct((ROWS, LANES), f32),
            jax.ShapeDtypeStruct((1, 1), f32),
        ),
        in_specs=[vmem, vmem],
        out_specs=(vmem, vmem),
        scratch_shapes=[
            pltpu.VMEM((len(SIDES), ROWS, LANES), f32),
            pltpu.VMEM((16, 1, LANES), f32),
            pltpu.SemaphoreType.DMA((len(SIDES),)),
            pltpu.SemaphoreType.DMA((len(SIDES),)),
            pltpu.SemaphoreType.DMA((16,)),
            pltpu.SemaphoreType.DMA((16,)),
        ],
        compiler_params=pltpu.CompilerParams(collective_id=0, has_side_effects=True),
    )(rhs, shares)


def solution(mesh):
    gx, gy = mesh.shape["gx"], mesh.shape["gy"]

    def shards(chem, temp, flow, counts, owners, weight, molar, factor, energy, release):
        chem_new, temp_new, rhs, shares = chemistry(
            chem, temp, flow, counts, owners, weight, molar, factor, energy, release
        )
        field, burden = project(rhs, shares, gx, gy)
        return chem_new, temp_new, field, burden

    return jax.shard_map(
        shards,
        mesh=mesh,
        in_specs=(
            P(None, "gx", "gy"),
            P("gx", "gy"),
            P("gx", "gy"),
            P("gx", "gy"),
            P("gx", "gy"),
            P(),
            P(),
            P(),
            P(),
            P(),
        ),
        out_specs=(P(None, "gx", "gy"), P("gx", "gy"), P("gx", "gy"), P("gx", "gy")),
        check_vma=False,
    )
```

time: 301 us -> 39.7 us (0.13)
  the two profiles are of different devices: /device:TPU:646 before, /device:TPU:2 now
where the time goes in v1:
time: 39.7 us; the launch traced here: 39.3 us
  Pallas kernels  35.6 us (90%)
  between operations  2.39 us (6%)
  local copies, waits for them, and re-layouts  1.32 us (3%)
    pallas_call x1, Pallas kernels, project(): pl.pallas_call(functools.partial(project_kernel, gx, gy), name='project',...  22.1 us
    pallas_call x1, Pallas kernels, chemistry(): pl.pallas_call(chemistry_kernel, name='chemistry', out_shape=(jax.ShapeDt...  13.5 us
    unnamed x1, local copies, waits for them, and re-layouts  1.32 us

profile of v1, /device:TPU:2, one launch (start us, length us, event | category | flops | bytes accessed | tf_op | source)
XLA Modules:
  0.0 39.3 jit_solution(8655832415712482669)
XLA Ops:
  0.6 13.5 %chemistry.1 = (f32[53,32,128]{2,1,0:T(8,128)}, f32[32,128]{1,0:T(8,128)}, f32[32,128]{1,0:T(8,128)}, f32[16,1,128]{2,1,0:T(1,128)}) custom-call(s32[1,16]{1,0:T(1,128)} %counts.1, s32[1,16]{1,0:T(1,128)} %owners.1, f32[53,32,128]{2,1,0:T(8,128)} %chem_hbm.1, f32[32,128]{1,0:T(8,128)} %temp_ref.1, f32[32,128]{1,0:T(8,128)} %flow_ref.1, f32[53,325]{1,0:T(8,128)} %bitcast.2, ...), custom_call_target="tpu_custom_call" | custom-call | tf_op jit(solution)/shard_map/chemistry/pallas_call | solution.py:161
  14.1 22.1 %project.1 = (f32[32,128]{1,0:T(8,128)}, f32[1,1]{1,0:T(1,128)}) custom-call(f32[32,128]{1,0:T(8,128)} %get-tuple-element.12.rhs_ref, f32[16,1,128]{2,1,0:T(1,128)} %get-tuple-element.13.share_ref), custom_call_target="tpu_custom_call" | custom-call | tf_op jit(solution)/shard_map/project/pallas_call | solution.py:352
  36.3 1.3 %copy.16 = f32[32,128]{1,0:T(8,128)} copy(f32[32,128]{1,0:T(8,128)} %get-tuple-element.22) | data formatting | bytes 32768

commit v2 on v1

v2 whole, which is shorter than its diff:
```python
import functools

import jax
import jax.numpy as jnp
from jax import lax
from jax.experimental import pallas as pl
from jax.experimental.pallas import tpu as pltpu
from jax.sharding import PartitionSpec as P

NS = 53
NR = 325
MAXSUB = 4
TILES = 16
ROWS = 32
LANES = 128
STATE = 64
REACT = 336
TEMP_ROW = 53
HEAT_ROW = 54
GROUPS = 4
STRIP = 32
GROUP_ROWS = ROWS // GROUPS
step_time = 0.4
MESH = pl.DeviceIdType.MESH
KEPT = pltpu.VMEM


def halves(x):
    top = x.astype(jnp.bfloat16)
    rest = (x - top.astype(jnp.float32)).astype(jnp.bfloat16)
    return top, rest


SIDES = tuple((a, b) for a in (-1, 0, 1) for b in (-1, 0, 1) if (a, b) != (0, 0))


def shifted(x, by, axis):
    return pltpu.roll(x, by % x.shape[axis], axis)


def beside(u, d):
    return (shifted(u, d, 0) + shifted(u, -d, 0)) + (shifted(u, d, 1) + shifted(u, -d, 1))


def pooled(x, d, row_first, lane_first):
    x = x + jnp.where(row_first, shifted(x, -d, 0), shifted(x, d, 0))
    return x + jnp.where(lane_first, shifted(x, -d, 1), shifted(x, d, 1))


def projection(rhs, inside):
    rows = lax.broadcasted_iota(jnp.int32, rhs.shape, 0)
    lanes = lax.broadcasted_iota(jnp.int32, rhs.shape, 1)
    weigh = jnp.where(inside, 0.2, 0.0)

    def sweep(u, f, d):
        return 0.2 * u + weigh * (f + beside(u, d))

    f0 = rhs
    u0 = sweep(weigh * f0, f0, 1)
    r0 = f0 - (4.0 * u0 - beside(u0, 1))
    f1 = pooled(r0, 1, (rows & 1) == 0, (lanes & 1) == 0)
    u1 = sweep(weigh * f1, f1, 2)
    r1 = f1 - (4.0 * u1 - beside(u1, 2))
    f2 = pooled(r1, 2, (rows & 2) == 0, (lanes & 2) == 0)
    u2 = weigh * f2
    for _ in range(3):
        u2 = sweep(u2, f2, 4)
    u1 = u1 + u2
    for _ in range(2):
        u1 = sweep(u1, f1, 2)
    u0 = u0 + u1
    for _ in range(2):
        u0 = sweep(u0, f0, 1)
    return u0


def peers(gx, gy):
    i = lax.axis_index("gx")
    j = lax.axis_index("gy")

    def there(a, b):
        here = [i + a >= 0] if a < 0 else [i + a < gx] if a > 0 else []
        here += [j + b >= 0] if b < 0 else [j + b < gy] if b > 0 else []
        return functools.reduce(jnp.logical_and, here)

    return i, j, there


def strip(block, start):
    lane = lax.broadcasted_iota(jnp.int32, (8, LANES), 1)
    packed = jnp.zeros((8, LANES), jnp.float32)
    for k in range(GROUPS):
        moved = pltpu.roll(block[8 * k : 8 * k + 8], (STRIP * k - start) % LANES, 1)
        packed = jnp.where((lane >= STRIP * k) & (lane < STRIP * (k + 1)), moved, packed)
    return packed


def react_kernel(
    gx,
    gy,
    counts,
    owners,
    chem_hbm,
    temp_hbm,
    flow_hbm,
    weight_hbm,
    molar_hbm,
    factor_ref,
    energy_ref,
    release_ref,
    out_buf,
    temp_out,
    rhs_ref,
    rows_in,
    strips_in,
    parts,
    chem_buf,
    temp_ref,
    flow_ref,
    weight_ref,
    molar_ref,
    state,
    wide,
    energy_cols,
    first,
    second,
    pad,
    strips,
    shares,
    in_sem,
    load_sem,
    send,
    recv,
    part_send,
    part_recv,
):
    i, j, there = peers(gx, gy)

    def fetch(g):
        return pltpu.make_async_copy(
            chem_hbm.at[:, pl.ds(g * GROUP_ROWS, GROUP_ROWS), :], chem_buf.at[g], in_sem.at[g]
        )

    loads = [
        pltpu.make_async_copy(source, target, load_sem.at[n])
        for n, (source, target) in enumerate(
            (
                (weight_hbm, weight_ref),
                (molar_hbm, molar_ref),
                (temp_hbm, temp_ref),
                (flow_hbm, flow_ref),
            )
        )
    ]
    for load in loads[:2]:
        load.start()
    for g in range(GROUPS):
        fetch(g).start()
    for load in loads[2:]:
        load.start()

    barrier = pltpu.get_barrier_semaphore()
    expected = jnp.int32(gx - 1)
    for d in range(1, gx):
        pl.semaphore_signal(
            barrier, inc=1, device_id={"gx": lax.rem(i + d, gx), "gy": j}, device_id_type=MESH
        )
    for a, b in SIDES:
        if b == 0:
            continue
        expected += there(a, b).astype(jnp.int32)

        @pl.when(there(a, b))
        def _(a=a, b=b):
            pl.semaphore_signal(
                barrier, inc=1, device_id={"gx": i + a, "gy": j + b}, device_id_type=MESH
            )

    pad[...] = jnp.zeros_like(pad)
    pad[0:1, 0:NR] = energy_ref[...].reshape(1, NR) * -1.4426950408889634
    columns = jnp.broadcast_to(pad[...], (LANES, 384)).T[0:REACT]
    energy_cols[:, 0:128] = columns
    energy_cols[:, 128:256] = columns
    wide[...] = jnp.zeros_like(wide)

    loads[0].wait()
    wide[0:NS, 0:NR] = weight_ref[...] * jnp.exp(factor_ref[...].reshape(1, NR))
    whole = wide[:, 0:384]
    top = whole.astype(jnp.bfloat16).astype(jnp.float32)
    both = jnp.concatenate([top, whole - top], axis=0).T[0:REACT].astype(jnp.bfloat16)
    first[:, 0:128] = both
    first[:, 128:256] = both

    loads[1].wait()
    wide[0:NS, 0:NR] = molar_ref[...]
    wide[TEMP_ROW : TEMP_ROW + 1, 0:NR] = release_ref[...].reshape(1, NR)
    wide[HEAT_ROW : HEAT_ROW + 1, 0:NR] = release_ref[...].reshape(1, NR)
    whole = wide[0:56, :]
    top = whole.astype(jnp.bfloat16).astype(jnp.float32)
    twice = top + pltpu.roll(top, REACT, 1)
    second[...] = jnp.concatenate([twice, whole - top], axis=0).astype(jnp.bfloat16)

    state[NS:STATE, :] = jnp.zeros((STATE - NS, ROWS * LANES), jnp.float32)
    for g in range(GROUPS):
        fetch(g).wait()
        rows = chem_buf.at[g].reshape(NS * GROUP_ROWS, LANES)
        for r in range(GROUP_ROWS):
            lanes = pl.ds((g * GROUP_ROWS + r) * LANES, LANES)
            state[0:NS, lanes] = rows[pl.ds(r, NS, stride=GROUP_ROWS), :]
    loads[2].wait()
    for r in range(ROWS):
        state[TEMP_ROW : TEMP_ROW + 1, r * LANES : (r + 1) * LANES] = temp_ref[r : r + 1, :]

    def turn_body(turn, carry):
        def before(t):
            now = state[:, t * 256 : (t + 1) * 256]
            top, rest = halves(now)
            taken = jnp.concatenate([top, top, rest, rest], axis=0)
            return jnp.dot(first[...], taken, preferred_element_type=jnp.float32)

        def after(t, progress):
            cells = pl.ds(t * 256, 256)
            inverse = 1.0 / (1.0 + jnp.abs(state[TEMP_ROW : TEMP_ROW + 1, cells]))
            flux = jnp.exp2(energy_cols[...] * inverse) * progress
            mixed = jnp.concatenate(halves(flux), axis=0)
            made = jnp.dot(second[:, 0:512], mixed[0:512], preferred_element_type=jnp.float32)
            more = jnp.dot(
                second[0:64, 512:672], mixed[512:672], preferred_element_type=jnp.float32
            )
            change = made[0:56] + made[56:112] + more[0:56]
            count = jnp.full((1, 256), counts[0, t], jnp.int32)
            width = step_time / count.astype(jnp.float32)
            delta = jnp.where(turn < count, width, 0.0)
            state[0:56, cells] += delta * change

        ahead = before(0)
        for t in range(TILES):
            progress = ahead
            if t + 1 < TILES:
                ahead = before(t + 1)
            after(t, progress)
        return carry

    lax.fori_loop(0, MAXSUB, turn_body, 0)

    loads[3].wait()
    place = lax.broadcasted_iota(jnp.int32, (TILES, LANES), 0)
    share = jnp.zeros((TILES, LANES), jnp.float32)
    for r in range(ROWS):
        lanes = slice(r * LANES, (r + 1) * LANES)
        heat = state[HEAT_ROW : HEAT_ROW + 1, lanes]
        rhs_ref[r : r + 1, :] = flow_ref[r : r + 1, :] + heat
        share += jnp.where(place == owners[0, r // 2], heat * heat, 0.0)
    for o in range(TILES):
        shares[o] = share[o : o + 1, :]
    block = rhs_ref[...]
    strips[0] = strip(block, 0)
    strips[1] = strip(block, LANES - STRIP)

    pl.semaphore_wait(barrier, expected)

    def halo(n):
        a, b = SIDES[n]
        slot = len(SIDES) - 1 - n
        return pltpu.make_async_remote_copy(
            src_ref=rhs_ref if b == 0 else strips.at[0 if b < 0 else 1],
            dst_ref=rows_in.at[0 if a > 0 else 1] if b == 0 else strips_in.at[slot],
            send_sem=send.at[n],
            recv_sem=recv.at[slot],
            device_id={"gx": i + a, "gy": j + b},
            device_id_type=MESH,
        )

    def part(d):
        peer = lax.rem(i + d, gx)
        return pltpu.make_async_remote_copy(
            src_ref=shares.at[peer],
            dst_ref=parts.at[d],
            send_sem=part_send.at[d],
            recv_sem=part_recv.at[d],
            device_id={"gx": peer, "gy": j},
            device_id_type=MESH,
        )

    for n in (0, 2, 5, 7, 1, 6, 3, 4):

        @pl.when(there(*SIDES[n]))
        def _(n=n):
            halo(n).start()

    for d in range(1, gx):
        part(d).start()

    parts[0] = shares[i]
    for r in range(ROWS):
        temp_out[r : r + 1, :] = state[TEMP_ROW : TEMP_ROW + 1, r * LANES : (r + 1) * LANES]
    for g in range(GROUPS):
        rows = out_buf.at[g].reshape(NS * GROUP_ROWS, LANES)
        for r in range(GROUP_ROWS):
            lanes = pl.ds((g * GROUP_ROWS + r) * LANES, LANES)
            rows[pl.ds(r, NS, stride=GROUP_ROWS), :] = state[0:NS, lanes]

    for n in range(len(SIDES)):
        @pl.when(there(*SIDES[n]))
        def _(n=n):
            halo(len(SIDES) - 1 - n).wait_recv()

    for d in range(1, gx):
        part(d).wait_recv()

    for n in range(len(SIDES)):

        @pl.when(there(*SIDES[n]))
        def _(n=n):
            halo(n).wait_send()

    for d in range(1, gx):
        part(d).wait_send()


def react(gx, gy, chem, temp, flow, counts, owners, weight, molar, factor, energy, release):
    vmem = pl.BlockSpec(memory_space=pltpu.VMEM)
    smem = pl.BlockSpec(memory_space=pltpu.SMEM)
    hbm = pl.BlockSpec(memory_space=pl.ANY)
    f32 = jnp.float32
    sides = len(SIDES)
    dma = pltpu.SemaphoreType.DMA
    return pl.pallas_call(
        functools.partial(react_kernel, gx, gy),
        name="react",
        out_shape=(
            KEPT((GROUPS, NS, GROUP_ROWS, LANES), f32),
            KEPT((ROWS, LANES), f32),
            KEPT((ROWS, LANES), f32),
            KEPT((2, ROWS, LANES), f32),
            KEPT((sides, 8, LANES), f32),
            KEPT((gx, 1, LANES), f32),
        ),
        in_specs=[smem, smem] + [hbm] * 5 + [vmem] * 3,
        out_specs=(vmem,) * 6,
        scratch_shapes=[
            pltpu.VMEM((GROUPS, NS, GROUP_ROWS, LANES), f32),
            pltpu.VMEM((ROWS, LANES), f32),
            pltpu.VMEM((ROWS, LANES), f32),
            pltpu.VMEM((NS, NR), f32),
            pltpu.VMEM((NS, NR), f32),
            pltpu.VMEM((STATE, ROWS * LANES), f32),
            pltpu.VMEM((STATE, 768), f32),
            pltpu.VMEM((REACT, 256), f32),
            pltpu.VMEM((REACT, 256), jnp.bfloat16),
            pltpu.VMEM((112, 768), jnp.bfloat16),
            pltpu.VMEM((1, 384), f32),
            pltpu.VMEM((2, 8, LANES), f32),
            pltpu.VMEM((TILES, 1, LANES), f32),
            dma((GROUPS,)),
            dma((4,)),
            dma((sides,)),
            dma((sides,)),
            dma((gx,)),
            dma((gx,)),
        ],
        compiler_params=pltpu.CompilerParams(collective_id=0, has_side_effects=True),
    )(counts, owners, chem, temp, flow, weight.T, molar.T, factor, energy, release)


def project_kernel(
    gx,
    gy,
    chem_ref,
    temp_ref,
    rhs_ref,
    rows_in,
    strips_in,
    parts,
    chem_out,
    temp_out,
    field_ref,
    burden_ref,
    sem,
):
    i, j, _ = peers(gx, gy)
    stores = [
        pltpu.make_async_copy(
            chem_ref.at[g], chem_out.at[:, pl.ds(g * GROUP_ROWS, GROUP_ROWS), :], sem.at[g]
        )
        for g in range(GROUPS)
    ]
    stores.append(pltpu.make_async_copy(temp_ref, temp_out, sem.at[GROUPS]))
    for store in stores:
        store.start()

    total = parts[0]
    for d in range(1, gx):
        total = total + parts[d]
    burden_ref[...] = jnp.sum(total, axis=1, keepdims=True) / float(ROWS * LANES)

    middle = jnp.concatenate([rows_in[0], rhs_ref[...], rows_in[1]], axis=0)
    middle = pltpu.roll(middle, 64, 1)

    def beside_column(b, at):
        column = []
        for a in (-1, 0, 1):
            packed = strips_in[SIDES.index((a, b))]
            column += [pltpu.roll(packed, (at - STRIP * k) % LANES, 1) for k in range(GROUPS)]
        return jnp.concatenate(column, axis=0)

    lane = lax.broadcasted_iota(jnp.int32, middle.shape, 1)
    left = jnp.where(lane < 64, beside_column(-1, STRIP), middle)
    right = jnp.where(lane < 64, middle, beside_column(1, 64))
    grid = jnp.concatenate([left, right], axis=1)
    rows = lax.broadcasted_iota(jnp.int32, grid.shape, 0)
    lanes = lax.broadcasted_iota(jnp.int32, grid.shape, 1)
    known = (lanes >= 64 - STRIP) & (lanes < 192 + STRIP)
    rows, lanes = rows + (i - 1) * ROWS, lanes + (j * LANES - 64)
    inside = (rows >= 0) & (rows < gx * ROWS) & (lanes >= 0) & (lanes < gy * LANES) & known
    field = projection(jnp.where(inside, grid, 0.0), inside)[ROWS : 2 * ROWS]
    left, right = pltpu.roll(field[:, 0:128], 64, 1), pltpu.roll(field[:, 128:256], 64, 1)
    lane = lax.broadcasted_iota(jnp.int32, left.shape, 1)
    field_ref[...] = jnp.where(lane < 64, left, right)
    for store in stores:
        store.wait()


def held(x):
    return pltpu.with_memory_space_constraint(x, pltpu.VMEM)


def project(gx, gy, *arrays):
    vmem = pl.BlockSpec(memory_space=pltpu.VMEM)
    hbm = pl.BlockSpec(memory_space=pl.ANY)
    f32 = jnp.float32
    return pl.pallas_call(
        functools.partial(project_kernel, gx, gy),
        name="project",
        out_shape=(
            jax.ShapeDtypeStruct((NS, ROWS, LANES), f32),
            jax.ShapeDtypeStruct((ROWS, LANES), f32),
            jax.ShapeDtypeStruct((ROWS, LANES), f32),
            jax.ShapeDtypeStruct((1, 1), f32),
        ),
        in_specs=[vmem] * len(arrays),
        out_specs=(hbm, hbm, vmem, vmem),
        scratch_shapes=[pltpu.SemaphoreType.DMA((GROUPS + 1,))],
    )(*(held(x) for x in arrays))


def solution(mesh):
    gx, gy = mesh.shape["gx"], mesh.shape["gy"]

    def shards(*args):
        return project(gx, gy, *react(gx, gy, *args))

    return jax.shard_map(
        shards,
        mesh=mesh,
        in_specs=(
            P(None, "gx", "gy"),
            P("gx", "gy"),
            P("gx", "gy"),
            P("gx", "gy"),
            P("gx", "gy"),
            P(),
            P(),
            P(),
            P(),
            P(),
        ),
        out_specs=(P(None, "gx", "gy"), P("gx", "gy"), P("gx", "gy"), P("gx", "gy")),
        check_vma=False,
    )
```

time: 39.7 us -> 31.9 us (0.80)
  Pallas kernels: 35.6 us -> 31.1 us
  between operations: 2.39 us -> 0.64 us
  local copies, waits for them, and re-layouts: 1.32 us -> 0 us
    pallas_call x1, Pallas kernels: 22.1 us -> 2.77 us  [project(): pl.pallas_call(functools.partial(project_kernel, gx, gy), name='project',...]
    pallas_call x1, Pallas kernels: 13.5 us -> 28.3 us  [react(): pl.pallas_call(functools.partial(react_kernel, gx, gy), name='react', out...]
    unnamed x1 -> x0, local copies, waits for them, and re-layouts: 1.32 us -> none
where the time goes in v2:
time: 31.9 us; the launch traced here: 31.7 us
  Pallas kernels  31.1 us (97%)
  between operations  0.64 us (2%)
    pallas_call x1, Pallas kernels, react(): pl.pallas_call(functools.partial(react_kernel, gx, gy), name='react', out...  28.3 us
    pallas_call x1, Pallas kernels, project(): pl.pallas_call(functools.partial(project_kernel, gx, gy), name='project',...  2.77 us

profile of v2, /device:TPU:2, one launch (start us, length us, event | category | flops | bytes accessed | tf_op | source)
XLA Modules:
  0.0 31.7 jit_solution(826937669837999008)
XLA Ops:
  0.6 28.3 %react.1 = (f32[4,53,8,128]{3,2,1,0:T(8,128)S(1)}, f32[32,128]{1,0:T(8,128)S(1)}, f32[32,128]{1,0:T(8,128)S(1)}, f32[2,32,128]{2,1,0:T(8,128)S(1)}, f32[8,8,128]{2,1,0:T(8,128)S(1)}, /*index=5*/f32[16,1,128]{2,1,0:T(1,128)S(1)}) custom-call(s32[1,16]{1,0:T(1,128)} %counts.1, s32[1,16]{1,0:T(1,128)} %owners.1, f32[53,32,128]{2,1,0:T(8,128)} %chem_hbm.1, ...), custom_call_target="tpu_custom_call" | custom-call | tf_op jit(solution)/shard_map/react/pallas_call | solution.py:328
  28.9 2.8 %project.1 = (f32[53,32,128]{2,1,0:T(8,128)}, f32[32,128]{1,0:T(8,128)}, f32[32,128]{1,0:T(8,128)}, f32[1,1]{1,0:T(1,128)}) custom-call(f32[4,53,8,128]{3,2,1,0:T(8,128)S(1)} %get-tuple-element.10.chem_ref, f32[32,128]{1,0:T(8,128)S(1)} %get-tuple-element.11.temp_ref, f32[32,128]{1,0:T(8,128)S(1)} %get-tuple-element.12.rhs_ref, ...), custom_call_target="tpu_custom_call" | custom-call | tf_op jit(solution)/shard_map/project/pallas_call | solution.py:432

commit v3 on v2

--- a/solution.py
+++ b/solution.py
@@ -15,6 +15,9 @@
 LANES = 128
 STATE = 64
 REACT = 336
+AHEAD = 2
+BEHIND = 0
+UNROLL = 1
 TEMP_ROW = 53
 HEAT_ROW = 54
 GROUPS = 4
@@ -52,26 +55,30 @@
     lanes = lax.broadcasted_iota(jnp.int32, rhs.shape, 1)
     weigh = jnp.where(inside, 0.2, 0.0)
 
-    def sweep(u, f, d):
-        return 0.2 * u + weigh * (f + beside(u, d))
+    def sweep(u, f, d, w):
+        return 0.2 * u + w * (f + beside(u, d))
 
     f0 = rhs
-    u0 = sweep(weigh * f0, f0, 1)
+    u0 = sweep(weigh * f0, f0, 1, weigh)
     r0 = f0 - (4.0 * u0 - beside(u0, 1))
     f1 = pooled(r0, 1, (rows & 1) == 0, (lanes & 1) == 0)
-    u1 = sweep(weigh * f1, f1, 2)
+    u1 = sweep(weigh * f1, f1, 2, weigh)
     r1 = f1 - (4.0 * u1 - beside(u1, 2))
     f2 = pooled(r1, 2, (rows & 2) == 0, (lanes & 2) == 0)
-    u2 = weigh * f2
-    for _ in range(3):
-        u2 = sweep(u2, f2, 4)
-    u1 = u1 + u2
+    u2 = sweep(weigh * f2, f2, 4, weigh)
+    u2, f2, w = u2[8:88], f2[8:88], weigh[8:88]
+    u2 = sweep(u2, f2, 4, w)
+    u2, f2, w = u2[8:72], f2[8:72], weigh[16:80]
+    u2 = sweep(u2, f2, 4, w)[8:56]
+    middle = slice(24, 72)
+    f0, f1, w = f0[middle], f1[middle], weigh[middle]
+    u1 = u1[middle] + u2
     for _ in range(2):
-        u1 = sweep(u1, f1, 2)
-    u0 = u0 + u1
+        u1 = sweep(u1, f1, 2, w)
+    u0 = u0[middle] + u1
     for _ in range(2):
-        u0 = sweep(u0, f0, 1)
-    return u0
+        u0 = sweep(u0, f0, 1, w)
+    return u0[8:40]
 
 
 def peers(gx, gy):
@@ -105,9 +112,9 @@
     flow_hbm,
     weight_hbm,
     molar_hbm,
-    factor_ref,
-    energy_ref,
-    release_ref,
+    factor_hbm,
+    energy_hbm,
+    release_hbm,
     out_buf,
     temp_out,
     rhs_ref,
@@ -119,6 +126,9 @@
     flow_ref,
     weight_ref,
     molar_ref,
+    factor_ref,
+    energy_ref,
+    release_ref,
     state,
     wide,
     energy_cols,
@@ -145,19 +155,26 @@
         pltpu.make_async_copy(source, target, load_sem.at[n])
         for n, (source, target) in enumerate(
             (
+                (energy_hbm, energy_ref),
+                (factor_hbm, factor_ref),
                 (weight_hbm, weight_ref),
+                (release_hbm, release_ref),
                 (molar_hbm, molar_ref),
                 (temp_hbm, temp_ref),
                 (flow_hbm, flow_ref),
             )
         )
     ]
-    for load in loads[:2]:
+    for load in loads[:5]:
         load.start()
     for g in range(GROUPS):
         fetch(g).start()
-    for load in loads[2:]:
+    for load in loads[5:]:
         load.start()
+
+    pad[...] = jnp.zeros_like(pad)
+    wide[...] = jnp.zeros_like(wide)
+    state[NS:STATE, :] = jnp.zeros((STATE - NS, ROWS * LANES), jnp.float32)
 
     barrier = pltpu.get_barrier_semaphore()
     expected = jnp.int32(gx - 1)
@@ -176,14 +193,14 @@
                 barrier, inc=1, device_id={"gx": i + a, "gy": j + b}, device_id_type=MESH
             )
 
-    pad[...] = jnp.zeros_like(pad)
+    loads[0].wait()
     pad[0:1, 0:NR] = energy_ref[...].reshape(1, NR) * -1.4426950408889634
     columns = jnp.broadcast_to(pad[...], (LANES, 384)).T[0:REACT]
     energy_cols[:, 0:128] = columns
     energy_cols[:, 128:256] = columns
-    wide[...] = jnp.zeros_like(wide)
-
-    loads[0].wait()
+
+    loads[1].wait()
+    loads[2].wait()
     wide[0:NS, 0:NR] = weight_ref[...] * jnp.exp(factor_ref[...].reshape(1, NR))
     whole = wide[:, 0:384]
     top = whole.astype(jnp.bfloat16).astype(jnp.float32)
@@ -191,7 +208,8 @@
     first[:, 0:128] = both
     first[:, 128:256] = both
 
-    loads[1].wait()
+    loads[3].wait()
+    loads[4].wait()
     wide[0:NS, 0:NR] = molar_ref[...]
     wide[TEMP_ROW : TEMP_ROW + 1, 0:NR] = release_ref[...].reshape(1, NR)
     wide[HEAT_ROW : HEAT_ROW + 1, 0:NR] = release_ref[...].reshape(1, NR)
@@ -200,50 +218,53 @@
     twice = top + pltpu.roll(top, REACT, 1)
     second[...] = jnp.concatenate([twice, whole - top], axis=0).astype(jnp.bfloat16)
 
-    state[NS:STATE, :] = jnp.zeros((STATE - NS, ROWS * LANES), jnp.float32)
     for g in range(GROUPS):
         fetch(g).wait()
         rows = chem_buf.at[g].reshape(NS * GROUP_ROWS, LANES)
         for r in range(GROUP_ROWS):
             lanes = pl.ds((g * GROUP_ROWS + r) * LANES, LANES)
             state[0:NS, lanes] = rows[pl.ds(r, NS, stride=GROUP_ROWS), :]
-    loads[2].wait()
+    loads[5].wait()
     for r in range(ROWS):
         state[TEMP_ROW : TEMP_ROW + 1, r * LANES : (r + 1) * LANES] = temp_ref[r : r + 1, :]
 
-    def turn_body(turn, carry):
-        def before(t):
-            now = state[:, t * 256 : (t + 1) * 256]
-            top, rest = halves(now)
-            taken = jnp.concatenate([top, top, rest, rest], axis=0)
-            return jnp.dot(first[...], taken, preferred_element_type=jnp.float32)
-
-        def after(t, progress):
-            cells = pl.ds(t * 256, 256)
-            inverse = 1.0 / (1.0 + jnp.abs(state[TEMP_ROW : TEMP_ROW + 1, cells]))
-            flux = jnp.exp2(energy_cols[...] * inverse) * progress
-            mixed = jnp.concatenate(halves(flux), axis=0)
-            made = jnp.dot(second[:, 0:512], mixed[0:512], preferred_element_type=jnp.float32)
-            more = jnp.dot(
-                second[0:64, 512:672], mixed[512:672], preferred_element_type=jnp.float32
-            )
-            change = made[0:56] + made[56:112] + more[0:56]
-            count = jnp.full((1, 256), counts[0, t], jnp.int32)
-            width = step_time / count.astype(jnp.float32)
-            delta = jnp.where(turn < count, width, 0.0)
-            state[0:56, cells] += delta * change
-
-        ahead = before(0)
-        for t in range(TILES):
-            progress = ahead
-            if t + 1 < TILES:
-                ahead = before(t + 1)
-            after(t, progress)
+    def before(step):
+        t = step % TILES
+        now = state[:, t * 256 : (t + 1) * 256]
+        top, rest = halves(now)
+        taken = jnp.concatenate([top, top, rest, rest], axis=0)
+        return jnp.dot(first[...], taken, preferred_element_type=jnp.float32)
+
+    def middle(step, progress):
+        t = step % TILES
+        inverse = 1.0 / (1.0 + jnp.abs(state[TEMP_ROW : TEMP_ROW + 1, t * 256 : (t + 1) * 256]))
+        flux = jnp.exp2(energy_cols[...] * inverse) * progress
+        mixed = jnp.concatenate(halves(flux), axis=0)
+        made = jnp.dot(second[:, 0:512], mixed[0:512], preferred_element_type=jnp.float32)
+        more = jnp.dot(second[0:64, 512:672], mixed[512:672], preferred_element_type=jnp.float32)
+        return made[0:56] + made[56:112] + more[0:56]
+
+    def finish(turn, step, change):
+        t = step % TILES
+        count = jnp.full((1, 256), counts[0, t], jnp.int32)
+        width = step_time / count.astype(jnp.float32)
+        delta = jnp.where(turn + step // TILES < count, width, 0.0)
+        state[0:56, t * 256 : (t + 1) * 256] += delta * change
+
+    def turn_body(index, carry):
+        ahead, made = {}, {}
+        for step in range(-AHEAD, UNROLL * TILES + BEHIND):
+            if step + AHEAD < UNROLL * TILES:
+                ahead[step + AHEAD] = before(step + AHEAD)
+            if 0 <= step < UNROLL * TILES:
+                made[step] = middle(step, ahead.pop(step))
+            if step >= BEHIND:
+                finish(index * UNROLL, step - BEHIND, made.pop(step - BEHIND))
         return carry
 
-    lax.fori_loop(0, MAXSUB, turn_body, 0)
-
-    loads[3].wait()
+    lax.fori_loop(0, MAXSUB // UNROLL, turn_body, 0)
+
+    loads[6].wait()
     place = lax.broadcasted_iota(jnp.int32, (TILES, LANES), 0)
     share = jnp.zeros((TILES, LANES), jnp.float32)
     for r in range(ROWS):
@@ -276,20 +297,20 @@
         return pltpu.make_async_remote_copy(
             src_ref=shares.at[peer],
             dst_ref=parts.at[d],
-            send_sem=part_send.at[d],
-            recv_sem=part_recv.at[d],
+            send_sem=part_send,
+            recv_sem=part_recv,
             device_id={"gx": peer, "gy": j},
             device_id_type=MESH,
         )
+
+    for d in range(1, gx):
+        part(d).start()
 
     for n in (0, 2, 5, 7, 1, 6, 3, 4):
 
         @pl.when(there(*SIDES[n]))
         def _(n=n):
             halo(n).start()
-
-    for d in range(1, gx):
-        part(d).start()
 
     parts[0] = shares[i]
     for r in range(ROWS):
@@ -305,8 +326,7 @@
         def _(n=n):
             halo(len(SIDES) - 1 - n).wait_recv()
 
-    for d in range(1, gx):
-        part(d).wait_recv()
+    pltpu.make_async_copy(parts.at[pl.ds(1, gx - 1)], parts.at[pl.ds(1, gx - 1)], part_recv).wait()
 
     for n in range(len(SIDES)):
 
@@ -314,8 +334,7 @@
         def _(n=n):
             halo(n).wait_send()
 
-    for d in range(1, gx):
-        part(d).wait_send()
+    pltpu.make_async_copy(shares.at[pl.ds(1, gx - 1)], shares.at[pl.ds(1, gx - 1)], part_send).wait()
 
 
 def react(gx, gy, chem, temp, flow, counts, owners, weight, molar, factor, energy, release):
@@ -336,7 +355,7 @@
             KEPT((sides, 8, LANES), f32),
             KEPT((gx, 1, LANES), f32),
         ),
-        in_specs=[smem, smem] + [hbm] * 5 + [vmem] * 3,
+        in_specs=[smem, smem] + [hbm] * 8,
         out_specs=(vmem,) * 6,
         scratch_shapes=[
             pltpu.VMEM((GROUPS, NS, GROUP_ROWS, LANES), f32),
@@ -344,6 +363,9 @@
             pltpu.VMEM((ROWS, LANES), f32),
             pltpu.VMEM((NS, NR), f32),
             pltpu.VMEM((NS, NR), f32),
+            pltpu.VMEM((NR,), f32),
+            pltpu.VMEM((NR,), f32),
+            pltpu.VMEM((NR,), f32),
             pltpu.VMEM((STATE, ROWS * LANES), f32),
             pltpu.VMEM((STATE, 768), f32),
             pltpu.VMEM((REACT, 256), f32),
@@ -353,11 +375,11 @@
             pltpu.VMEM((2, 8, LANES), f32),
             pltpu.VMEM((TILES, 1, LANES), f32),
             dma((GROUPS,)),
-            dma((4,)),
+            dma((7,)),
             dma((sides,)),
             dma((sides,)),
-            dma((gx,)),
-            dma((gx,)),
+            dma(()),
+            dma(()),
         ],
         compiler_params=pltpu.CompilerParams(collective_id=0, has_side_effects=True),
     )(counts, owners, chem, temp, flow, weight.T, molar.T, factor, energy, release)
@@ -413,7 +435,7 @@
     known = (lanes >= 64 - STRIP) & (lanes < 192 + STRIP)
     rows, lanes = rows + (i - 1) * ROWS, lanes + (j * LANES - 64)
     inside = (rows >= 0) & (rows < gx * ROWS) & (lanes >= 0) & (lanes < gy * LANES) & known
-    field = projection(jnp.where(inside, grid, 0.0), inside)[ROWS : 2 * ROWS]
+    field = projection(jnp.where(inside, grid, 0.0), inside)
     left, right = pltpu.roll(field[:, 0:128], 64, 1), pltpu.roll(field[:, 128:256], 64, 1)
     lane = lax.broadcasted_iota(jnp.int32, left.shape, 1)
     field_ref[...] = jnp.where(lane < 64, left, right)

time: 31.9 us -> 29.5 us (0.925)
  Pallas kernels: 31.1 us -> 28.7 us
    pallas_call x1, Pallas kernels: 28.3 us -> 26.1 us  [react(): pl.pallas_call(functools.partial(react_kernel, gx, gy), name='react', out...]
where the time goes in v3:
time: 29.5 us; the launch traced here: 29.4 us
  Pallas kernels  28.7 us (97%)
  between operations  0.64 us (2%)
    pallas_call x1, Pallas kernels, react(): pl.pallas_call(functools.partial(react_kernel, gx, gy), name='react', out...  26.1 us
    pallas_call x1, Pallas kernels, project(): pl.pallas_call(functools.partial(project_kernel, gx, gy), name='project',...  2.61 us

profile of v3, /device:TPU:2, one launch (start us, length us, event | category | flops | bytes accessed | tf_op | source)
XLA Modules:
  0.0 29.4 jit_solution(126358109938186009)
XLA Ops:
  0.6 26.1 %react.1 = (f32[4,53,8,128]{3,2,1,0:T(8,128)S(1)}, f32[32,128]{1,0:T(8,128)S(1)}, f32[32,128]{1,0:T(8,128)S(1)}, f32[2,32,128]{2,1,0:T(8,128)S(1)}, f32[8,8,128]{2,1,0:T(8,128)S(1)}, /*index=5*/f32[16,1,128]{2,1,0:T(1,128)S(1)}) custom-call(s32[1,16]{1,0:T(1,128)} %counts.1, s32[1,16]{1,0:T(1,128)} %owners.1, f32[53,32,128]{2,1,0:T(8,128)} %chem_hbm.1, ...), custom_call_target="tpu_custom_call" | custom-call | tf_op jit(solution)/shard_map/react/pallas_call | solution.py:347
  26.8 2.6 %project.1 = (f32[53,32,128]{2,1,0:T(8,128)}, f32[32,128]{1,0:T(8,128)}, f32[32,128]{1,0:T(8,128)}, f32[1,1]{1,0:T(1,128)}) custom-call(f32[4,53,8,128]{3,2,1,0:T(8,128)S(1)} %get-tuple-element.10.chem_ref, f32[32,128]{1,0:T(8,128)S(1)} %get-tuple-element.11.temp_ref, f32[32,128]{1,0:T(8,128)S(1)} %get-tuple-element.12.rhs_ref, ...), custom_call_target="tpu_custom_call" | custom-call | tf_op jit(solution)/shard_map/project/pallas_call | solution.py:454

commit v4 on v3

--- a/solution.py
+++ b/solution.py
@@ -16,8 +16,6 @@
 STATE = 64
 REACT = 336
 AHEAD = 2
-BEHIND = 0
-UNROLL = 1
 TEMP_ROW = 53
 HEAT_ROW = 54
 GROUPS = 4
@@ -135,6 +133,7 @@
     first,
     second,
     pad,
+    widths,
     strips,
     shares,
     in_sem,
@@ -176,6 +175,12 @@
     wide[...] = jnp.zeros_like(wide)
     state[NS:STATE, :] = jnp.zeros((STATE - NS, ROWS * LANES), jnp.float32)
 
+    turns = lax.broadcasted_iota(jnp.int32, (8, 256), 0)
+    for t in range(TILES):
+        count = jnp.full((8, 256), counts[0, t], jnp.int32)
+        width = step_time / count.astype(jnp.float32)
+        widths[:, t * 256 : (t + 1) * 256] = jnp.where(turns < count, width, 0.0)
+
     barrier = pltpu.get_barrier_semaphore()
     expected = jnp.int32(gx - 1)
     for d in range(1, gx):
@@ -218,15 +223,14 @@
     twice = top + pltpu.roll(top, REACT, 1)
     second[...] = jnp.concatenate([twice, whole - top], axis=0).astype(jnp.bfloat16)
 
-    for g in range(GROUPS):
+    def take(g):
         fetch(g).wait()
         rows = chem_buf.at[g].reshape(NS * GROUP_ROWS, LANES)
         for r in range(GROUP_ROWS):
             lanes = pl.ds((g * GROUP_ROWS + r) * LANES, LANES)
             state[0:NS, lanes] = rows[pl.ds(r, NS, stride=GROUP_ROWS), :]
-    loads[5].wait()
-    for r in range(ROWS):
-        state[TEMP_ROW : TEMP_ROW + 1, r * LANES : (r + 1) * LANES] = temp_ref[r : r + 1, :]
+            row = g * GROUP_ROWS + r
+            state[TEMP_ROW : TEMP_ROW + 1, lanes] = temp_ref[row : row + 1, :]
 
     def before(step):
         t = step % TILES
@@ -244,34 +248,31 @@
         more = jnp.dot(second[0:64, 512:672], mixed[512:672], preferred_element_type=jnp.float32)
         return made[0:56] + made[56:112] + more[0:56]
 
-    def finish(turn, step, change):
-        t = step % TILES
-        count = jnp.full((1, 256), counts[0, t], jnp.int32)
-        width = step_time / count.astype(jnp.float32)
-        delta = jnp.where(turn + step // TILES < count, width, 0.0)
-        state[0:56, t * 256 : (t + 1) * 256] += delta * change
-
-    def turn_body(index, carry):
-        ahead, made = {}, {}
-        for step in range(-AHEAD, UNROLL * TILES + BEHIND):
-            if step + AHEAD < UNROLL * TILES:
-                ahead[step + AHEAD] = before(step + AHEAD)
-            if 0 <= step < UNROLL * TILES:
-                made[step] = middle(step, ahead.pop(step))
-            if step >= BEHIND:
-                finish(index * UNROLL, step - BEHIND, made.pop(step - BEHIND))
-        return carry
-
-    lax.fori_loop(0, MAXSUB // UNROLL, turn_body, 0)
-
-    loads[6].wait()
+    def finish(step, change):
+        turn, t = divmod(step, TILES)
+        cells = slice(t * 256, (t + 1) * 256)
+        state[0:56, cells] += widths[turn : turn + 1, cells] * change
+
     place = lax.broadcasted_iota(jnp.int32, (TILES, LANES), 0)
     share = jnp.zeros((TILES, LANES), jnp.float32)
-    for r in range(ROWS):
-        lanes = slice(r * LANES, (r + 1) * LANES)
-        heat = state[HEAT_ROW : HEAT_ROW + 1, lanes]
-        rhs_ref[r : r + 1, :] = flow_ref[r : r + 1, :] + heat
-        share += jnp.where(place == owners[0, r // 2], heat * heat, 0.0)
+    steps = MAXSUB * TILES
+    ahead = {}
+    loads[5].wait()
+    loads[6].wait()
+    for step in range(-AHEAD, steps):
+        if step + AHEAD < steps:
+            group, rest = divmod(step + AHEAD, TILES // GROUPS)
+            if group < GROUPS and rest == 0:
+                take(group)
+            ahead[step + AHEAD] = before(step + AHEAD)
+        if step >= 0:
+            finish(step, middle(step, ahead.pop(step)))
+        if step >= steps - TILES:
+            t = step % TILES
+            for r in (2 * t, 2 * t + 1):
+                heat = state[HEAT_ROW : HEAT_ROW + 1, r * LANES : (r + 1) * LANES]
+                rhs_ref[r : r + 1, :] = flow_ref[r : r + 1, :] + heat
+                share += jnp.where(place == owners[0, t], heat * heat, 0.0)
     for o in range(TILES):
         shares[o] = share[o : o + 1, :]
     block = rhs_ref[...]
@@ -372,6 +373,7 @@
             pltpu.VMEM((REACT, 256), jnp.bfloat16),
             pltpu.VMEM((112, 768), jnp.bfloat16),
             pltpu.VMEM((1, 384), f32),
+            pltpu.VMEM((8, ROWS * LANES), f32),
             pltpu.VMEM((2, 8, LANES), f32),
             pltpu.VMEM((TILES, 1, LANES), f32),
             dma((GROUPS,)),

time: 29.5 us -> 28.8 us (0.976)
  Pallas kernels: 28.7 us -> 27.9 us
    pallas_call x1, Pallas kernels: 26.1 us -> 25.3 us  [react(): pl.pallas_call(functools.partial(react_kernel, gx, gy), name='react', out...]
where the time goes in v4:
time: 28.8 us; the launch traced here: 28.6 us
  Pallas kernels  27.9 us (97%)
  between operations  0.64 us (2%)
    pallas_call x1, Pallas kernels, react(): pl.pallas_call(functools.partial(react_kernel, gx, gy), name='react', out...  25.3 us
    pallas_call x1, Pallas kernels, project(): pl.pallas_call(functools.partial(project_kernel, gx, gy), name='project',...  2.61 us

profile of v4, /device:TPU:2, one launch (start us, length us, event | category | flops | bytes accessed | tf_op | source)
XLA Modules:
  0.0 28.6 jit_solution(12084787656074950418)
XLA Ops:
  0.6 25.3 %react.1 = (f32[4,53,8,128]{3,2,1,0:T(8,128)S(1)}, f32[32,128]{1,0:T(8,128)S(1)}, f32[32,128]{1,0:T(8,128)S(1)}, f32[2,32,128]{2,1,0:T(8,128)S(1)}, f32[8,8,128]{2,1,0:T(8,128)S(1)}, /*index=5*/f32[16,1,128]{2,1,0:T(1,128)S(1)}) custom-call(s32[1,16]{1,0:T(1,128)} %counts.1, s32[1,16]{1,0:T(1,128)} %owners.1, f32[53,32,128]{2,1,0:T(8,128)} %chem_hbm.1, ...), custom_call_target="tpu_custom_call" | custom-call | tf_op jit(solution)/shard_map/react/pallas_call | solution.py:348
  25.9 2.6 %project.1 = (f32[53,32,128]{2,1,0:T(8,128)}, f32[32,128]{1,0:T(8,128)}, f32[32,128]{1,0:T(8,128)}, f32[1,1]{1,0:T(1,128)}) custom-call(f32[4,53,8,128]{3,2,1,0:T(8,128)S(1)} %get-tuple-element.10.chem_ref, f32[32,128]{1,0:T(8,128)S(1)} %get-tuple-element.11.temp_ref, f32[32,128]{1,0:T(8,128)S(1)} %get-tuple-element.12.rhs_ref, ...), custom_call_target="tpu_custom_call" | custom-call | tf_op jit(solution)/shard_map/project/pallas_call | solution.py:456

commit v5 on v4

--- a/solution.py
+++ b/solution.py
@@ -275,10 +275,6 @@
                 share += jnp.where(place == owners[0, t], heat * heat, 0.0)
     for o in range(TILES):
         shares[o] = share[o : o + 1, :]
-    block = rhs_ref[...]
-    strips[0] = strip(block, 0)
-    strips[1] = strip(block, LANES - STRIP)
-
     pl.semaphore_wait(barrier, expected)
 
     def halo(n):
@@ -304,14 +300,20 @@
             device_id_type=MESH,
         )
 
+    def send_to(*order):
+        for n in order:
+
+            @pl.when(there(*SIDES[n]))
+            def _(n=n):
+                halo(n).start()
+
+    send_to(1, 6)
     for d in range(1, gx):
         part(d).start()
-
-    for n in (0, 2, 5, 7, 1, 6, 3, 4):
-
-        @pl.when(there(*SIDES[n]))
-        def _(n=n):
-            halo(n).start()
+    block = rhs_ref[...]
+    strips[0] = strip(block, 0)
+    strips[1] = strip(block, LANES - STRIP)
+    send_to(0, 2, 5, 7, 3, 4)
 
     parts[0] = shares[i]
     for r in range(ROWS):

time: 28.8 us -> 28.9 us (level)
  no operation moved by 1% of the time
where the time goes in v5:
time: 28.9 us; the launch traced here: 28.5 us
  Pallas kernels  27.9 us (97%)
  between operations  0.64 us (2%)
    pallas_call x1, Pallas kernels, react(): pl.pallas_call(functools.partial(react_kernel, gx, gy), name='react', out...  25.2 us
    pallas_call x1, Pallas kernels, project(): pl.pallas_call(functools.partial(project_kernel, gx, gy), name='project',...  2.61 us

profile of v5, /device:TPU:2, one launch (start us, length us, event | category | flops | bytes accessed | tf_op | source)
XLA Modules:
  0.0 28.5 jit_solution(4945854815458800517)
XLA Ops:
  0.6 25.2 %react.1 = (f32[4,53,8,128]{3,2,1,0:T(8,128)S(1)}, f32[32,128]{1,0:T(8,128)S(1)}, f32[32,128]{1,0:T(8,128)S(1)}, f32[2,32,128]{2,1,0:T(8,128)S(1)}, f32[8,8,128]{2,1,0:T(8,128)S(1)}, /*index=5*/f32[16,1,128]{2,1,0:T(1,128)S(1)}) custom-call(s32[1,16]{1,0:T(1,128)} %counts.1, s32[1,16]{1,0:T(1,128)} %owners.1, f32[53,32,128]{2,1,0:T(8,128)} %chem_hbm.1, ...), custom_call_target="tpu_custom_call" | custom-call | tf_op jit(solution)/shard_map/react/pallas_call | solution.py:350
  25.9 2.6 %project.1 = (f32[53,32,128]{2,1,0:T(8,128)}, f32[32,128]{1,0:T(8,128)}, f32[32,128]{1,0:T(8,128)}, f32[1,1]{1,0:T(1,128)}) custom-call(f32[4,53,8,128]{3,2,1,0:T(8,128)S(1)} %get-tuple-element.10.chem_ref, f32[32,128]{1,0:T(8,128)S(1)} %get-tuple-element.11.temp_ref, f32[32,128]{1,0:T(8,128)S(1)} %get-tuple-element.12.rhs_ref, ...), custom_call_target="tpu_custom_call" | custom-call | tf_op jit(solution)/shard_map/project/pallas_call | solution.py:458
